TPU v7x, 128 devices: a whole 4x4x4 slice. The times are simulated.
128 devices in a mesh: row: 16 (over y, z), col: 8 (over x, core).
Axes of the slice: x: 4, y: 4, z: 4, core: 2. Of those that a mesh axis runs over, the one named last changes fastest.
Arguments:
- node_latent: bfloat16 [32768, 512], P(('row', 'col')), may hold values from -6 to 6
- edge_latent: bfloat16 [262144, 512], P(('row', 'col')), may hold values from -6 to 6
- node_cotangent: bfloat16 [32768, 512], P(('row', 'col')), may hold values from -6 to 6
- edge_cotangent: bfloat16 [262144, 512], P(('row', 'col')), may hold values from -6 to 6
- w_edge_in: bfloat16 [1536, 512], replicated, may hold values from -0.15625 to 0.15625
- w_edge_out: bfloat16 [512, 512], replicated, may hold values from -0.25 to 0.25
- w_node_in: bfloat16 [1024, 512], replicated, may hold values from -0.1875 to 0.1875
- w_node_out: bfloat16 [512, 512], replicated, may hold values from -0.25 to 0.25
- sender_code: int32 [262144], P(('row', 'col')), may hold values from 0 to 1535, as said below
- receiver: int32 [262144], P(('row', 'col')), may hold values from 0 to 255
- near_list: int32 [128, 4, 64], P(('row', 'col')), may hold values from 0 to 255
- far_list: int32 [128, 128, 8], P(('row', 'col')), may hold values from 0 to 255
Outputs:
- node_new: bfloat16 [32768, 512], P(('row', 'col'))
- edge_new: bfloat16 [262144, 512], P(('row', 'col'))
- grad_node: bfloat16 [32768, 512], P(('row', 'col'))
- grad_edge: bfloat16 [262144, 512], P(('row', 'col'))
- grad_edge_in: float32 [1536, 512], P(('row', 'col'))
- grad_edge_out: float32 [512, 512], P(('row', 'col'))
- grad_node_in: float32 [1024, 512], P(('row', 'col'))
- grad_node_out: float32 [512, 512], P(('row', 'col'))
Inputs may be any that keep to these rules, and one draw needn't show every extreme that they name: `sender_code`: for each block d and each device p, the far codes of block d that name p use the first c of the 8 slots, 1 <= c <= 8, c drawn for each pair, and every block uses all 8 slots of some device. Every local code, every near code and every used far code is read by at least one edge of its block.
All inputs are finite; a program needn't handle non-finite values.
Results may differ from a plain program's by a relative error of at most 0.015.
Values may be sent and summed in bfloat16 or wider, within the bound.
No kernel may reach another device: no remote copies, remote signals or barrier semaphores. Data moves between devices by JAX's collectives and lax.ppermute only.
A program may use at most 128 MiB of HBM per device.

v0:
```python
import math

import jax
import jax.numpy as jnp
from jax import lax
from jax.sharding import PartitionSpec as P

EPS = 1e-05


def passed_along(value, axis, by):
    peers = lax.axis_size(axis)
    return lax.ppermute(value, axis, [(i, (i + by) % peers) for i in range(peers)])


def shortened(value):
    return jax.tree.map(lambda a: a.astype(jnp.bfloat16) if a.dtype == jnp.float32 else a, value)


def in_blocks(value, dim, peers):
    dims = value.shape
    blocks = value.reshape(*dims[:dim], peers, dims[dim] // peers, *dims[dim + 1 :])
    return jnp.moveaxis(blocks, dim, 0)


def sum_at_owner(value, axis, dim):
    peers = lax.axis_size(axis)
    blocks = lax.all_to_all(in_blocks(value, dim, peers), axis, 0, 0, tiled=True)
    return jnp.sum(blocks.astype(jnp.float32), axis=0)


def layer_norm(value):
    mean = jnp.mean(value, -1, keepdims=True)
    centred = value - mean
    recip = lax.rsqrt(jnp.mean(centred * centred, -1, keepdims=True) + EPS)
    return centred * recip


def norm_grad(value, grad):
    mean = jnp.mean(value, -1, keepdims=True)
    centred = value - mean
    recip = lax.rsqrt(jnp.mean(centred * centred, -1, keepdims=True) + EPS)
    normed = centred * recip
    inner = (
        grad
        - jnp.mean(grad, -1, keepdims=True)
        - normed * jnp.mean(grad * normed, -1, keepdims=True)
    )
    return recip * inner


def silu_grad(value):
    sigma = jax.nn.sigmoid(value)
    return sigma * (1.0 + value * (1.0 - sigma))


def plain_dot(left, right):
    return jnp.dot(left, right, preferred_element_type=jnp.float32)


def exact_dot(left, right):
    return jnp.dot(left, right, preferred_element_type=jnp.float32)


def back_dot(left, weight):
    return lax.dot_general(
        left, weight, (((1,), (1,)), ((), ())), preferred_element_type=jnp.float32
    )


def exact_back(left, weight):
    return lax.dot_general(
        left,
        weight.astype(jnp.float32),
        (((1,), (1,)), ((), ())),
        preferred_element_type=jnp.float32,
    )


def cross_dot(left, right):
    return lax.dot_general(
        left, right, (((0,), (0,)), ((), ())), preferred_element_type=jnp.float32
    )


def shards(
    node_latent,
    edge_latent,
    node_cotangent,
    edge_cotangent,
    w_edge_in,
    w_edge_out,
    w_node_in,
    w_node_out,
    sender_code,
    receiver,
    near_list,
    far_list,
):
    node_rows, width = node_latent.shape
    edge_rows = edge_latent.shape[0]
    rows_grid = lax.axis_size("row")
    cols_grid = lax.axis_size("col")
    peers = rows_grid * cols_grid
    near_lists = near_list[0]
    far_lists = far_list[0]
    near_width = near_lists.shape[1]
    far_width = far_lists.shape[1]
    steps_row = ((0, 1), (1, -1))
    steps_col = ((2, 1), (3, -1))
    near_send = jnp.take(node_latent, near_lists, axis=0)
    near_parts = []
    for slot_index, offset in steps_row:
        near_parts.append(passed_along(near_send[slot_index], "row", offset))
    for slot_index, offset in steps_col:
        near_parts.append(passed_along(near_send[slot_index], "col", offset))
    far_send = jnp.take(node_latent, far_lists, axis=0)
    far_recv = lax.all_to_all(far_send, ("row", "col"), split_axis=0, concat_axis=0, tiled=True)
    far_recv = far_recv.reshape(peers * far_width, width)
    table = jnp.concatenate([node_latent] + near_parts + [far_recv], 0)
    table_rows = table.shape[0]
    w_e = w_edge_in[:width]
    w_s = w_edge_in[width : 2 * width]
    w_r = w_edge_in[2 * width :]
    sent_rows = jnp.take(table, sender_code, axis=0)
    recv_rows = jnp.take(node_latent, receiver, axis=0)
    edge_pre = plain_dot(edge_latent, w_e) + plain_dot(sent_rows, w_s) + plain_dot(recv_rows, w_r)
    edge_hidden = jax.nn.silu(edge_pre).astype(jnp.bfloat16)
    edge_mid = plain_dot(edge_hidden, w_edge_out)
    edge_new = (edge_latent.astype(jnp.float32) + layer_norm(edge_mid)).astype(jnp.bfloat16)
    node_ids = jnp.arange(node_rows, dtype=jnp.int32)[:, None]
    onehot = (receiver[None, :] == node_ids).astype(jnp.bfloat16)
    gathered = plain_dot(onehot, edge_new).astype(jnp.bfloat16)
    node_pre = plain_dot(node_latent, w_node_in[:width]) + plain_dot(gathered, w_node_in[width:])
    node_hidden = jax.nn.silu(node_pre).astype(jnp.bfloat16)
    node_mid = plain_dot(node_hidden, w_node_out)
    node_new = (node_latent.astype(jnp.float32) + layer_norm(node_mid)).astype(jnp.bfloat16)
    node_delta = norm_grad(node_mid, node_cotangent.astype(jnp.float32)).astype(jnp.bfloat16)
    node_pre_delta = (back_dot(node_delta, w_node_out) * silu_grad(node_pre)).astype(jnp.bfloat16)
    gathered_grad = back_dot(node_pre_delta, w_node_in[width:])
    node_in_grad = back_dot(node_pre_delta, w_node_in[:width])
    grad_node_in = jnp.concatenate(
        [cross_dot(node_latent, node_pre_delta), cross_dot(gathered, node_pre_delta)], 0
    )
    grad_node_out = cross_dot(node_hidden, node_delta)
    edge_total = edge_cotangent.astype(jnp.float32) + jnp.take(gathered_grad, receiver, axis=0)
    edge_delta = norm_grad(edge_mid, edge_total).astype(jnp.bfloat16)
    edge_pre_delta = (back_dot(edge_delta, w_edge_out) * silu_grad(edge_pre)).astype(jnp.bfloat16)
    grad_edge = (edge_total + back_dot(edge_pre_delta, w_e)).astype(jnp.bfloat16)
    grad_edge_in = jnp.concatenate(
        [
            cross_dot(edge_latent, edge_pre_delta),
            cross_dot(sent_rows, edge_pre_delta),
            cross_dot(recv_rows, edge_pre_delta),
        ],
        0,
    )
    grad_edge_out = cross_dot(edge_hidden, edge_delta)
    code_ids = jnp.arange(table_rows, dtype=jnp.int32)[:, None]
    code_onehot = (sender_code[None, :] == code_ids).astype(jnp.bfloat16)
    code_sums = plain_dot(code_onehot, edge_pre_delta)
    table_grad = exact_back(code_sums, w_s)
    recv_sums = plain_dot(onehot, edge_pre_delta)
    node_total = node_cotangent.astype(jnp.float32) + node_in_grad + table_grad[:node_rows]
    node_total = node_total + exact_back(recv_sums, w_r)
    near_grad = table_grad[node_rows : node_rows + 4 * near_width].reshape(4, near_width, width)
    returned_parts = []
    for slot_index, offset in steps_row:
        returned_parts.append(
            passed_along(near_grad[slot_index].astype(jnp.bfloat16), "row", -offset).astype(
                jnp.float32
            )
        )
    for slot_index, offset in steps_col:
        returned_parts.append(
            passed_along(near_grad[slot_index].astype(jnp.bfloat16), "col", -offset).astype(
                jnp.float32
            )
        )
    far_grad = table_grad[node_rows + 4 * near_width :].reshape(peers, far_width, width)
    far_back = lax.all_to_all(
        far_grad.astype(jnp.bfloat16), ("row", "col"), split_axis=0, concat_axis=0, tiled=True
    ).astype(far_grad.dtype)
    far_back = far_back.reshape(peers * far_width, width)
    returned_rows = jnp.concatenate(returned_parts + [far_back], 0)
    owner_index = jnp.concatenate([near_lists.reshape(-1), far_lists.reshape(-1)], 0)
    owner_onehot = (owner_index[None, :] == node_ids).astype(jnp.float32)
    node_total = node_total + exact_dot(owner_onehot, returned_rows)
    grad_node = node_total.astype(jnp.bfloat16)
    edge_scale = 1.0 / math.sqrt(edge_rows * peers)
    node_scale = 1.0 / math.sqrt(node_rows * peers)
    grads = (
        grad_edge_in * edge_scale,
        grad_edge_out * edge_scale,
        grad_node_in * node_scale,
        grad_node_out * node_scale,
    )
    shaped = tuple(
        (item.reshape(rows_grid, cols_grid, item.shape[0] // peers, width) for item in grads)
    )
    partial_sums = jax.tree.map(
        lambda part: part.astype(jnp.float32),
        lax.psum_scatter(shortened(shaped), "col", scatter_dimension=1, tiled=True),
    )
    summed = jax.tree.map(lambda part: sum_at_owner(part, "row", 0), shortened(partial_sums))
    summed = tuple((item.reshape(item.shape[2], width) for item in summed))
    return (node_new, edge_new, grad_node, grad_edge, summed[0], summed[1], summed[2], summed[3])


def solution(mesh):
    in_specs = (
        P(("row", "col"), None),
        P(("row", "col"), None),
        P(("row", "col"), None),
        P(("row", "col"), None),
        P(),
        P(),
        P(),
        P(),
        P(("row", "col")),
        P(("row", "col")),
        P(("row", "col"), None, None),
        P(("row", "col"), None, None),
    )
    out_specs = (
        P(("row", "col"), None),
        P(("row", "col"), None),
        P(("row", "col"), None),
        P(("row", "col"), None),
        P(("row", "col"), None),
        P(("row", "col"), None),
        P(("row", "col"), None),
        P(("row", "col"), None),
    )
    return jax.shard_map(shards, mesh=mesh, in_specs=in_specs, out_specs=out_specs, check_vma=False)
```

profile of v0, /device:TPU:0, one launch (start us, length us, event | category | flops | bytes accessed | tf_op | source)
XLA Modules:
  0.0 285.0 jit_solution(14384873315422316115)
XLA Ops:
  14.1 4.7 %collective-permute-start.1 = (bf16[64,512]{1,0:T(8,128)(2,1)S(1)}, bf16[64,512]{1,0:T(8,128)(2,1)S(1)}, u32[]{:S(2)}, u32[]{:S(2)}) collective-permute-start(bf16[64,512]{1,0:T(8,128)(2,1)S(1)} %get-tuple-element.44), channel_id=1, source_target_pairs={{0,120},{8,0},{16,8},{24,16},{32,24},{40,32},{48,40},{56,48},{64,5... | collective-permute-start | bytes 196616 | tf_op jit(solution)/shard_map/ppermute | solution.py:13
  27.0 5.8 %all-to-all-start = ((bf16[128,8,512]{2,1,0:T(8,128)(2,1)}), bf16[128,8,512]{2,1,0:T(8,128)(2,1)}, u32[]{:S(2)}, u32[]{:S(2)}) async-start(bf16[128,8,512]{2,1,0:T(8,128)(2,1)} %bitcast_select_fusion), calls=%async_computation | async-start | bytes 2097152 | tf_op jit(solution)/shard_map/all_to_all | solution.py:118
  33.4 9.2 %gather_fusion.3 = bf16[2048,512]{1,0:T(8,128)(2,1)} fusion(bf16[256,512]{1,0:T(8,128)(2,1)S(1)} %copy-done.1, s32[2048]{0:T(1024)S(1)} %fusion.44), kind=kCustom, calls=%fused_computation.3 | custom fusion | bytes 4202496 | tf_op jit(solution)/shard_map/jit(_take)/gather | solution.py:126
  42.6 4.1 %copy.44 = bf16[2048,512]{0,1:T(8,128)(2,1)} copy(bf16[2048,512]{1,0:T(8,128)(2,1)} %gather_fusion.3) | data formatting | bytes 4194304 | tf_op jit(solution)/shard_map/jit(_take)/gather | solution.py:126
  55.0 4.9 %fusion.38 = f32[2048,512]{1,0:T(8,128)} fusion(bf16[2048,512]{1,0:T(8,128)(2,1)} %param.13, bf16[1536,512]{1,0:T(8,128)(2,1)} %param.16), kind=kOutput, calls=%fused_computation.81 | convolution fusion | flops 1073741824 | bytes 6815744 | tf_op jit(solution)/shard_map/dot_general | solution.py:58
  61.3 9.2 %gather_fusion.2 = bf16[2048,512]{1,0:T(8,128)(2,1)} fusion(bf16[1536,512]{1,0:T(8,128)(2,1)S(1)} %bitcast_dynamic-update-slice_fusion.1, s32[2048]{0:T(1024)S(1)} %fusion.43), kind=kCustom, calls=%fused_computation.2 | custom fusion | bytes 4202496 | tf_op jit(solution)/shard_map/jit(_take)/gather | solution.py:125
  70.5 4.1 %copy.43 = bf16[2048,512]{0,1:T(8,128)(2,1)} copy(bf16[2048,512]{1,0:T(8,128)(2,1)} %gather_fusion.2) | data formatting | bytes 4194304 | tf_op jit(solution)/shard_map/jit(_take)/gather | solution.py:125
  78.0 4.2 %multiply_convert_fusion.2 = (bf16[2048,512]{1,0:T(8,128)(2,1)S(1)}, f32[2048,512]{1,0:T(8,128)}) fusion(bf16[1536,512]{1,0:T(8,128)(2,1)S(1)} %copy-done.22, bf16[2048,512]{0,1:T(8,128)(2,1)S(1)} %copy-done.15, pred[2048]{0:T(1024)(128)(4,1)S(1)} %compare_and_fusion, f32[2048,512]{1,0:T(8,128)S(1)} %copy-done.10, f32[2048,512]{1,0:T(8,128)S(1)} %fusion.7), kind=kOutput, calls=%fused_computation.15 | convolution fusion | flops 1082130432 | bytes 17303552 | tf_op jit(solution)/shard_map/dot_general | solution.py:58
  95.3 8.9 %gather_fusion.4 = f32[2048,512]{1,0:T(8,128)} fusion(f32[256,512]{1,0:T(8,128)S(1)} %fusion.30, s32[2048]{0:T(1024)S(1)} %fusion.44), kind=kCustom, calls=%fused_computation.4 | custom fusion | bytes 8396800 | tf_op jit(solution)/shard_map/jit(_take)/gather | solution.py:146
  104.2 5.5 %copy.46 = f32[2048,512]{0,1:T(8,128)} copy(f32[2048,512]{1,0:T(8,128)} %gather_fusion.4) | data formatting | bytes 8388608 | tf_op jit(solution)/shard_map/jit(_take)/gather | solution.py:146
  109.8 4.9 %fusion.50 = (f32[2048]{0:T(1024)S(1)}, f32[2048]{0:T(1024)S(1)}) fusion(f32[2048,512]{0,1:T(8,128)} %copy.46, pred[2048]{0:T(1024)(128)(4,1)S(1)} %compare_and_fusion, bf16[2048,512]{0,1:T(8,128)(2,1)S(1)} %copy-done.5, f32[2048]{0:T(1024)S(1)} %add_rsqrt_fusion, f32[2048,512]{0,1:T(8,128)} %copy-done.2, f32[2048]{0:T(1024)S(1)} %broadcast_multiply_fusion.2), kind=kLoop, calls=%fused_computation.132 | loop fusion | flops 8384512 | bytes 10520576 | tf_op jit(solution)/shard_map/reduce_sum | solution.py:46
  123.8 4.3 %fusion.12 = bf16[512,512]{1,0:T(8,128)(2,1)} fusion(bf16[2048,512]{1,0:T(8,128)(2,1)} %copy-done.11, bf16[2048,512]{0,1:T(8,128)(2,1)} %multiply_convert_fusion.1), kind=kOutput, calls=%fused_computation.39 | convolution fusion | flops 1074266112 | bytes 4718592 | tf_op jit(solution)/shard_map/dot_general | solution.py:81
  132.3 5.4 %multiply_convert_fusion = bf16[2048,512]{1,0:T(8,128)(2,1)S(1)} fusion(f32[2048,512]{1,0:T(8,128)} %get-tuple-element.47, bf16[2048,512]{0,1:T(8,128)(2,1)} %multiply_convert_fusion.1, bf16[512,512]{1,0:T(8,128)(2,1)S(1)} %copy-done), kind=kOutput, calls=%fused_computation.9 | convolution fusion | flops 1083179008 | bytes 8912896 | tf_op jit(solution)/shard_map/dot_general | solution.py:66
  155.7 8.1 %fusion.54 = (bf16[1536,512]{1,0:T(8,128)(2,1)}, f32[1536,512]{1,0:T(8,128)}) fusion(bf16[1536,512]{1,0:T(8,128)(2,1)} %param.16, bf16[2048,512]{1,0:T(8,128)(2,1)} %copy-done.18, s32[2048]{0:T(1024)S(1)} %copy-done.26), kind=kOutput, calls=%fused_computation.136 | convolution fusion | flops 4030464000 | bytes 7348224 | tf_op jit(solution)/shard_map/dot_general | solution.py:72
  166.3 5.0 %add_convert_fusion = bf16[2048,512]{0,1:T(8,128)(2,1)} fusion(bf16[2048,512]{1,0:T(8,128)(2,1)S(1)} %copy-done.20, bf16[1536,512]{1,0:T(8,128)(2,1)} %param.16, f32[2048,512]{0,1:T(8,128)} %copy.46, pred[2048]{0:T(1024)(128)(4,1)S(1)} %compare_and_fusion, bf16[2048,512]{0,1:T(8,128)(2,1)S(1)} %copy-done.5), kind=kOutput, calls=%fused_computation.8 | convolution fusion | flops 1078984704 | bytes 11012096 | tf_op jit(solution)/shard_map/dot_general | solution.py:66
  173.5 6.7 %all-to-all-start.4 = ((bf16[16,1,1,8,512]{4,3,2,1,0:T(8,128)(2,1)}), bf16[16,1,1,8,512]{4,3,2,1,0:T(8,128)(2,1)S(1)}, u32[]{:S(2)}, u32[]{:S(2)}) async-start(bf16[16,1,1,8,512]{4,3,2,1,0:T(8,128)(2,1)} %dynamic-slice_bitcast_fusion), calls=%async_computation.6 | async-start | bytes 262144 | tf_op jit(solution)/shard_map/all_to_all | solution.py:28
  181.8 5.2 %collective-permute-start.4 = (bf16[64,512]{1,0:T(8,128)(2,1)}, bf16[64,512]{1,0:T(8,128)(2,1)S(1)}, u32[]{:S(2)}, u32[]{:S(2)}) collective-permute-start(bf16[64,512]{1,0:T(8,128)(2,1)} %get-tuple-element.39), channel_id=1, source_target_pairs={{0,120},{8,0},{16,8},{24,16},{32,24},{40,32},{48,40},{56,48},{64,5... | collective-permute-start | bytes 196616 | tf_op jit(solution)/shard_map/ppermute | solution.py:13
  188.0 7.2 %all-to-all-start.1 = ((bf16[128,8,512]{2,1,0:T(8,128)(2,1)}), bf16[128,8,512]{2,1,0:T(8,128)(2,1)}, u32[]{:S(2)}, u32[]{:S(2)}) async-start(bf16[128,8,512]{2,1,0:T(8,128)(2,1)} %slice_bitcast_fusion), calls=%async_computation.1 | async-start | bytes 2097152 | tf_op jit(solution)/shard_map/all_to_all | solution.py:181
  209.9 5.0 %collective-permute-done.5 = bf16[64,512]{1,0:T(8,128)(2,1)S(1)} collective-permute-done((bf16[64,512]{1,0:T(8,128)(2,1)S(1)}, bf16[64,512]{1,0:T(8,128)(2,1)S(1)}, u32[]{:S(2)}, u32[]{:S(2)}) %collective-permute-start.5) | collective-permute-done | bytes 65568 | tf_op jit(solution)/shard_map/ppermute | solution.py:13
  217.2 7.1 %all-to-all-start.5 = ((bf16[16,1,1,4,512]{4,3,2,1,0:T(4,128)(2,1)}), bf16[16,1,1,4,512]{4,3,2,1,0:T(4,128)(2,1)S(1)}, u32[]{:S(2)}, u32[]{:S(2)}) async-start(bf16[16,1,1,4,512]{4,3,2,1,0:T(4,128)(2,1)} %copy.55), calls=%async_computation.8 | async-start | bytes 131072 | tf_op jit(solution)/shard_map/all_to_all | solution.py:28
  227.1 4.8 %all-to-all-done.5 = bf16[16,1,1,4,512]{4,3,2,1,0:T(4,128)(2,1)S(1)} async-done(((bf16[16,1,1,4,512]{4,3,2,1,0:T(4,128)(2,1)}), bf16[16,1,1,4,512]{4,3,2,1,0:T(4,128)(2,1)S(1)}, u32[]{:S(2)}, u32[]{:S(2)}) %all-to-all-start.5) | async-done | bytes 65568 | tf_op jit(solution)/shard_map/all_to_all | solution.py:28
  236.7 23.5 %reduce-scatter.5.cloned.1.call-done = bf16[16,1,12,512]{3,0,2,1:T(8,128)(2,1)} async-done(((bf16[16,8,12,512]{3,0,2,1:T(8,128)(2,1)}), bf16[16,1,12,512]{3,0,2,1:T(8,128)(2,1)}) %reduce-scatter.5.cloned.1.call-update) | async-done | bytes 196624 | tf_op jit(solution)/shard_map/reduce_scatter | solution.py:203
  261.9 7.0 %all-to-all-start.2 = ((bf16[16,1,1,12,512]{4,3,2,1,0:T(8,128)(2,1)}), bf16[16,1,1,12,512]{4,3,2,1,0:T(8,128)(2,1)S(1)}, u32[]{:S(2)}, u32[]{:S(2)}) async-start(bf16[16,1,1,12,512]{4,3,2,1,0:T(8,128)(2,1)} %copy.50), calls=%async_computation.3 | async-start | bytes 524288 | tf_op jit(solution)/shard_map/all_to_all | solution.py:28
  270.2 7.2 %all-to-all-done.2 = bf16[16,1,1,12,512]{4,3,2,1,0:T(8,128)(2,1)S(1)} async-done(((bf16[16,1,1,12,512]{4,3,2,1,0:T(8,128)(2,1)}), bf16[16,1,1,12,512]{4,3,2,1,0:T(8,128)(2,1)S(1)}, u32[]{:S(2)}, u32[]{:S(2)}) %all-to-all-start.2) | async-done | bytes 196640 | tf_op jit(solution)/shard_map/all_to_all | solution.py:28
  (182 shorter events, 108.3 us)
Async XLA Ops:
  7.2 75.1 %copy-start = (bf16[512,512]{1,0:T(8,128)(2,1)S(1)}, bf16[512,512]{1,0:T(8,128)(2,1)}, u32[]{:S(2)}) copy-start(bf16[512,512]{1,0:T(8,128)(2,1)} %param.17) | copy-start | bytes 1572868
  7.2 14.5 %copy-start.25 = (s32[1,128,8]{1,2,0:T(8,128)S(1)}, s32[1,128,8]{1,2,0:T(8,128)}, u32[]{:S(2)}) copy-start(s32[1,128,8]{1,2,0:T(8,128)} %param.23) | copy-start | bytes 12292
  7.2 14.5 %copy-start.1 = (bf16[256,512]{1,0:T(8,128)(2,1)S(1)}, bf16[256,512]{1,0:T(8,128)(2,1)}, u32[]{:S(2)}) copy-start(bf16[256,512]{1,0:T(8,128)(2,1)} %param.12) | copy-start | bytes 786436
  12.0 47.9 %collective-permute-start = (bf16[64,512]{1,0:T(8,128)(2,1)S(1)}, bf16[64,512]{1,0:T(8,128)(2,1)S(1)}, u32[]{:S(2)}, u32[]{:S(2)}) collective-permute-start(bf16[64,512]{1,0:T(8,128)(2,1)S(1)} %get-tuple-element.45), channel_id=1, source_target_pairs={{0,8},{8,16},{16,24},{24,32},{32,40},{40,48},{48,56},{56,64},{64,7... | collective-permute-start | bytes 196616 | tf_op jit(solution)/shard_map/ppermute | solution.py:13
  14.1 45.9 %collective-permute-start.1 = (bf16[64,512]{1,0:T(8,128)(2,1)S(1)}, bf16[64,512]{1,0:T(8,128)(2,1)S(1)}, u32[]{:S(2)}, u32[]{:S(2)}) collective-permute-start(bf16[64,512]{1,0:T(8,128)(2,1)S(1)} %get-tuple-element.44), channel_id=1, source_target_pairs={{0,120},{8,0},{16,8},{24,16},{32,24},{40,32},{48,40},{56,48},{64,5... | collective-permute-start | bytes 196616 | tf_op jit(solution)/shard_map/ppermute | solution.py:13
  18.7 41.2 %collective-permute-start.2 = (bf16[64,512]{1,0:T(8,128)(2,1)S(1)}, bf16[64,512]{1,0:T(8,128)(2,1)S(1)}, u32[]{:S(2)}, u32[]{:S(2)}) collective-permute-start(bf16[64,512]{1,0:T(8,128)(2,1)S(1)} %get-tuple-element.43), channel_id=1, source_target_pairs={{0,1},{1,2},{2,3},{3,4},{4,5},{5,6},{6,7},{7,0},{8,9},{9,10},{10,1... | collective-permute-start | bytes 196616 | tf_op jit(solution)/shard_map/ppermute | solution.py:13
  18.7 41.3 %collective-permute-start.3 = (bf16[64,512]{1,0:T(8,128)(2,1)S(1)}, bf16[64,512]{1,0:T(8,128)(2,1)S(1)}, u32[]{:S(2)}, u32[]{:S(2)}) collective-permute-start(bf16[64,512]{1,0:T(8,128)(2,1)S(1)} %get-tuple-element.42), channel_id=1, source_target_pairs={{0,7},{1,0},{2,1},{3,2},{4,3},{5,4},{6,5},{7,6},{8,15},{9,8},{10,9... | collective-permute-start | bytes 196616 | tf_op jit(solution)/shard_map/ppermute | solution.py:13
  25.8 7.5 %copy-start.28 = (s32[1,4,64]{2,1,0:T(4,128)S(1)}, s32[1,4,64]{2,1,0:T(4,128)}, u32[]{:S(2)}) copy-start(s32[1,4,64]{2,1,0:T(4,128)} %param.22) | copy-start | bytes 3076
  27.0 33.0 %all-to-all-start = ((bf16[128,8,512]{2,1,0:T(8,128)(2,1)}), bf16[128,8,512]{2,1,0:T(8,128)(2,1)}, u32[]{:S(2)}, u32[]{:S(2)}) async-start(bf16[128,8,512]{2,1,0:T(8,128)(2,1)} %bitcast_select_fusion), calls=%async_computation | async-start | bytes 2097152 | tf_op jit(solution)/shard_map/all_to_all | solution.py:118
  32.9 138.4 %all-reduce.3.cloned.1.call-start = ((), (), s32[]{:S(2)}) async-start(), calls=%async_computation.12 | async-start | bytes 2097152
  33.1 41.4 %copy-start.29 = (pred[2048]{0:T(1024)(128)(4,1)}, pred[2048]{0:T(1024)(128)(4,1)S(1)}, u32[]{:S(2)}) copy-start(pred[2048]{0:T(1024)(128)(4,1)S(1)} %compare_and_fusion.1) | copy-start | bytes 6148
  95.0 120.6 %reduce-scatter.9.cloned.1.call-start = ((), (), s32[]{:S(2)}) async-start(), calls=%async_computation.11 | async-start | bytes 589824 | tf_op jit(solution)/shard_map/reduce_scatter | solution.py:203
  132.2 93.4 %reduce-scatter.7.cloned.1.call-start = ((), (), s32[]{:S(2)}) async-start(), calls=%async_computation.10 | async-start | bytes 589824 | tf_op jit(solution)/shard_map/reduce_scatter | solution.py:203
  141.4 118.8 %reduce-scatter.5.cloned.1.call-start = ((), (), s32[]{:S(2)}) async-start(), calls=%async_computation.9 | async-start | bytes 1769472 | tf_op jit(solution)/shard_map/reduce_scatter | solution.py:203
  171.2 24.0 %copy-start.13 = (bf16[1024,512]{1,0:T(8,128)(2,1)S(1)}, bf16[1024,512]{1,0:T(8,128)(2,1)}, u32[]{:S(2)}) copy-start(bf16[1024,512]{1,0:T(8,128)(2,1)} %param.18) | copy-start | bytes 3145732
  173.5 14.5 %all-to-all-start.4 = ((bf16[16,1,1,8,512]{4,3,2,1,0:T(8,128)(2,1)}), bf16[16,1,1,8,512]{4,3,2,1,0:T(8,128)(2,1)S(1)}, u32[]{:S(2)}, u32[]{:S(2)}) async-start(bf16[16,1,1,8,512]{4,3,2,1,0:T(8,128)(2,1)} %dynamic-slice_bitcast_fusion), calls=%async_computation.6 | async-start | bytes 262144 | tf_op jit(solution)/shard_map/all_to_all | solution.py:28
  181.8 28.2 %collective-permute-start.4 = (bf16[64,512]{1,0:T(8,128)(2,1)}, bf16[64,512]{1,0:T(8,128)(2,1)S(1)}, u32[]{:S(2)}, u32[]{:S(2)}) collective-permute-start(bf16[64,512]{1,0:T(8,128)(2,1)} %get-tuple-element.39), channel_id=1, source_target_pairs={{0,120},{8,0},{16,8},{24,16},{32,24},{40,32},{48,40},{56,48},{64,5... | collective-permute-start | bytes 196616 | tf_op jit(solution)/shard_map/ppermute | solution.py:13
  188.0 29.1 %all-to-all-start.1 = ((bf16[128,8,512]{2,1,0:T(8,128)(2,1)}), bf16[128,8,512]{2,1,0:T(8,128)(2,1)}, u32[]{:S(2)}, u32[]{:S(2)}) async-start(bf16[128,8,512]{2,1,0:T(8,128)(2,1)} %slice_bitcast_fusion), calls=%async_computation.1 | async-start | bytes 2097152 | tf_op jit(solution)/shard_map/all_to_all | solution.py:181
  206.7 8.2 %collective-permute-start.5 = (bf16[64,512]{1,0:T(8,128)(2,1)S(1)}, bf16[64,512]{1,0:T(8,128)(2,1)S(1)}, u32[]{:S(2)}, u32[]{:S(2)}) collective-permute-start(bf16[64,512]{1,0:T(8,128)(2,1)S(1)} %get-tuple-element.38), channel_id=1, source_target_pairs={{0,8},{8,16},{16,24},{24,32},{32,40},{40,48},{48,56},{56,64},{64,7... | collective-permute-start | bytes 196616 | tf_op jit(solution)/shard_map/ppermute | solution.py:13
  207.7 7.2 %collective-permute-start.6 = (bf16[64,512]{1,0:T(8,128)(2,1)S(1)}, bf16[64,512]{1,0:T(8,128)(2,1)S(1)}, u32[]{:S(2)}, u32[]{:S(2)}) collective-permute-start(bf16[64,512]{1,0:T(8,128)(2,1)S(1)} %get-tuple-element.37), channel_id=1, source_target_pairs={{0,7},{1,0},{2,1},{3,2},{4,3},{5,4},{6,5},{7,6},{8,15},{9,8},{10,9... | collective-permute-start | bytes 196616 | tf_op jit(solution)/shard_map/ppermute | solution.py:13
  209.9 5.1 %collective-permute-start.7 = (bf16[64,512]{1,0:T(8,128)(2,1)S(1)}, bf16[64,512]{1,0:T(8,128)(2,1)S(1)}, u32[]{:S(2)}, u32[]{:S(2)}) collective-permute-start(bf16[64,512]{1,0:T(8,128)(2,1)S(1)} %get-tuple-element.36), channel_id=1, source_target_pairs={{0,1},{1,2},{2,3},{3,4},{4,5},{5,6},{6,7},{7,0},{8,9},{9,10},{10,1... | collective-permute-start | bytes 196616 | tf_op jit(solution)/shard_map/ppermute | solution.py:13
  217.2 14.8 %all-to-all-start.5 = ((bf16[16,1,1,4,512]{4,3,2,1,0:T(4,128)(2,1)}), bf16[16,1,1,4,512]{4,3,2,1,0:T(4,128)(2,1)S(1)}, u32[]{:S(2)}, u32[]{:S(2)}) async-start(bf16[16,1,1,4,512]{4,3,2,1,0:T(4,128)(2,1)} %copy.55), calls=%async_computation.8 | async-start | bytes 131072 | tf_op jit(solution)/shard_map/all_to_all | solution.py:28
  232.0 29.9 %all-to-all-start.3 = ((bf16[16,1,1,4,512]{4,3,2,1,0:T(4,128)(2,1)}), bf16[16,1,1,4,512]{4,3,2,1,0:T(4,128)(2,1)S(1)}, u32[]{:S(2)}, u32[]{:S(2)}) async-start(bf16[16,1,1,4,512]{4,3,2,1,0:T(4,128)(2,1)} %copy.52), calls=%async_computation.5 | async-start | bytes 131072 | tf_op jit(solution)/shard_map/all_to_all | solution.py:28
  261.9 15.5 %all-to-all-start.2 = ((bf16[16,1,1,12,512]{4,3,2,1,0:T(8,128)(2,1)}), bf16[16,1,1,12,512]{4,3,2,1,0:T(8,128)(2,1)S(1)}, u32[]{:S(2)}, u32[]{:S(2)}) async-start(bf16[16,1,1,12,512]{4,3,2,1,0:T(8,128)(2,1)} %copy.50), calls=%async_computation.3 | async-start | bytes 524288 | tf_op jit(solution)/shard_map/all_to_all | solution.py:28
  (27 other events, 98.4 us)
Sparse Core Ops, SparseCore 0:
  95.1 63.5 all-reduce.2
  161.1 30.8 reduce-scatter.8
  194.3 31.1 reduce-scatter.6
  227.8 32.3 reduce-scatter.4
where the time goes:
time: 290 us; the launch traced here: 285 us
  local copies, waits for them, and re-layouts  97.7 us (34%)
  starting transfers between devices  56.2 us (19%)
  matrix products  55 us (19%)
  waiting for transfers between devices  41.6 us (14%)
  other arithmetic  19.5 us (7%)
  between operations  14.9 us (5%)
    all_to_all x4, starting transfers between devices, sum_at_owner(): lax.all_to_all(in_blocks(value, dim, peers), axis, 0, 0, tiled=True)  24.3 us
    reduce_scatter x3, waiting for transfers between devices, shards(): lax.psum_scatter(shortened(shaped), 'col', scatter_dimension=1, tiled=True)  23.5 us
    unnamed x81, local copies, waits for them, and re-layouts  20.8 us
    ppermute x8, starting transfers between devices, passed_along(): lax.ppermute(value, axis, [(i, (i + by) % peers) for i in range(peers)])  18.1 us
    dot_general x8, matrix products, plain_dot(): return jnp.dot(left, right, preferred_element_type=jnp.float32)  16.2 us
    convert_element_type x6, local copies, waits for them, and re-layouts, shortened(): a.astype(jnp.bfloat16)  15.6 us
    gather x2, local copies, waits for them, and re-layouts, shards(): jnp.take(gathered_grad, receiver, axis=0)  14.5 us
    dot_general x7, matrix products, cross_dot(): lax.dot_general(left, right, (((0,), (0,)), ((), ())), preferred_element_...  13.4 us
  transfers between devices with their start and end apart: 18, of which 6 were waited for; matrix products, arithmetic and copies ran while one was open for 45% of the time, Pallas kernels for 0%

commit v1 on v0

v1 whole, which is shorter than its diff:
```python
import functools
import math

import jax
import jax.numpy as jnp
from jax import lax
from jax.experimental import pallas as pl
from jax.experimental.pallas import tpu as pltpu
from jax.sharding import PartitionSpec as P


EPS = 1e-05
BF = jnp.bfloat16
F32 = jnp.float32
AXES = ("row", "col")
D = 512
VMEM_LIMIT = 60 * 1024 * 1024


def dot(left, right):
    return jnp.dot(left, right, preferred_element_type=F32)


def dot_nt(left, right):
    return lax.dot_general(left, right, (((1,), (1,)), ((), ())), preferred_element_type=F32)


def dot_tn(left, right):
    return lax.dot_general(left, right, (((0,), (0,)), ((), ())), preferred_element_type=F32)


def iota(shape, dim):
    return lax.broadcasted_iota(jnp.int32, shape, dim)


def hot(mask):
    return jnp.where(mask, 1.0, 0.0).astype(BF)


def normed(value):
    mean = jnp.mean(value, -1, keepdims=True)
    centred = value - mean
    recip = lax.rsqrt(jnp.mean(centred * centred, -1, keepdims=True) + EPS)
    return centred * recip, recip


def norm_grad(y, recip, grad):
    inner = grad - jnp.mean(grad, -1, keepdims=True) - y * jnp.mean(grad * y, -1, keepdims=True)
    return recip * inner


def full(shape):
    return pl.BlockSpec(shape, lambda *_: (0,) * len(shape))


def params():
    return pltpu.CompilerParams(
        dimension_semantics=("arbitrary",), vmem_limit_bytes=VMEM_LIMIT
    )


def cost(flops, nbytes):
    return pl.CostEstimate(flops=int(flops), bytes_accessed=int(nbytes), transcendentals=0)


def column_of(table, groups, width):
    rows = groups * width
    pick = hot(iota((rows, groups), 0) // width == iota((rows, groups), 1))
    spread = dot(pick, table.astype(F32).astype(BF))
    keep = iota((rows, width), 0) % width == iota((rows, width), 1)
    return jnp.sum(jnp.where(keep, spread, 0.0), -1, keepdims=True).astype(jnp.int32)


def offer_kernel(node_ref, near_ref, far_ref, near_out, far_out):
    node = node_ref[...]
    rows = node.shape[0]
    near = near_ref[0]
    far = far_ref[0]
    near_col = column_of(near, *near.shape)
    far_col = column_of(far, *far.shape)
    n_near, n_far = near_col.shape[0], far_col.shape[0]
    far_out[...] = dot(hot(far_col == iota((n_far, rows), 1)), node).astype(BF)
    near_out[...] = dot(hot(near_col == iota((n_near, rows), 1)), node).astype(BF)


def local_kernel(
    rows, edge_ref, node_ref, we_ref, ws_ref, wr_ref, code_c, code_r, recv_c, recv_r,
    p_out, oh_out, oht_out, ohr_out, ohrt_out, nwr, nws,
):
    @pl.when(pl.program_id(0) == 0)
    def _():
        node = node_ref[...]
        nwr[...] = dot(node, wr_ref[...]).astype(BF)
        nws[...] = dot(node, ws_ref[...]).astype(BF)

    tile = edge_ref.shape[0]
    code = code_c[...]
    ohr = hot(recv_c[...] == iota((tile, rows), 1))
    ohl = hot(code == iota((tile, rows), 1))
    p_out[...] = dot(edge_ref[...], we_ref[...]) + dot(ohr, nwr[...]) + dot(ohl, nws[...])
    ohr_out[...] = ohr
    oh_out[...] = hot(code - rows == iota(oh_out.shape, 1))
    oht_out[...] = hot(code_r[...] == iota(oht_out.shape, 0))
    ohrt_out[...] = hot(recv_r[...] == iota(ohrt_out.shape, 0))


def main_kernel(
    steps, p_ref, oh_ref, edge_ref, ohrt_ref, cot_ref, ohr_ref, ohtf_ref,
    n0, n1, n2, n3, far_ref, ws_ref, wo_ref,
    node_ref, ncot_ref, va_ref, vb_ref, vo_ref,
    enew_out, nnew_out, epd_out, hid_out, ed_out, gg_out, fgrad_out, cs_out,
    ntot_out, gat_out, npd_out, nhid_out, nd_out,
    tws, acc, y_s, sp_s, rec_s, cs,
):
    step = pl.program_id(0)
    tile = edge_ref.shape[0]

    @pl.when(step == 0)
    def _():
        ws = ws_ref[...]
        width = n0.shape[0]
        for k, ref in enumerate((n0, n1, n2, n3)):
            tws[k * width : (k + 1) * width, :] = dot(ref[...], ws).astype(BF)
        tws[4 * width :, :] = dot(far_ref[...], ws).astype(BF)
        acc[...] = jnp.zeros_like(acc)

    @pl.when(step < steps)
    def _():
        pre = p_ref[...] + dot(oh_ref[...], tws[...])
        sigma = jax.nn.sigmoid(pre)
        hidden = pre * sigma
        sp = sigma + hidden * (1.0 - sigma)
        hid = hidden.astype(BF)
        mid = dot(hid, wo_ref[...])
        y, rec = normed(mid)
        enew = (edge_ref[...].astype(F32) + y).astype(BF)
        enew_out[...] = enew
        acc[...] += dot(ohrt_ref[...], enew)
        hid_out[pl.ds(step * tile, tile), :] = hid
        y_s[pl.ds(step * tile, tile), :] = y.astype(BF)
        sp_s[pl.ds(step * tile, tile), :] = sp.astype(BF)
        rec_s[pl.ds(step * tile, tile), :] = rec

    @pl.when(step == steps)
    def _():
        node = node_ref[...]
        gat = acc[...].astype(BF)
        pre = dot(node, va_ref[...]) + dot(gat, vb_ref[...])
        sigma = jax.nn.sigmoid(pre)
        hidden = pre * sigma
        hid = hidden.astype(BF)
        mid = dot(hid, vo_ref[...])
        y, rec = normed(mid)
        nnew_out[...] = (node.astype(F32) + y).astype(BF)
        ncot = ncot_ref[...].astype(F32)
        nd = norm_grad(y, rec, ncot).astype(BF)
        npd = (dot_nt(nd, vo_ref[...]) * (sigma + hidden * (1.0 - sigma))).astype(BF)
        gg_out[...] = dot_nt(npd, vb_ref[...]).astype(BF)
        ntot_out[...] = ncot + dot_nt(npd, va_ref[...])
        gat_out[...] = gat
        npd_out[...] = npd
        nhid_out[...] = hid
        nd_out[...] = nd
        cs[...] = jnp.zeros_like(cs)

    @pl.when(step >= steps)
    def _():
        at = (step - steps) * tile
        total = cot_ref[...].astype(F32) + dot(ohr_ref[...], gg_out[...])
        y = y_s[pl.ds(at, tile), :].astype(F32)
        ed = norm_grad(y, rec_s[pl.ds(at, tile), :], total).astype(BF)
        ed_out[...] = ed
        sp = sp_s[pl.ds(at, tile), :].astype(F32)
        epd = (dot_nt(ed, wo_ref[...]) * sp).astype(BF)
        epd_out[...] = epd
        cs[...] += dot(ohtf_ref[...], epd)

    @pl.when(step == 2 * steps - 1)
    def _():
        sums = cs[...].astype(BF)
        cs_out[...] = sums
        fgrad_out[...] = dot_nt(sums, ws_ref[...]).astype(BF)


def rest_kernel(
    steps, core_ref, edge_ref, cot_ref, ohr_ref, ohrt_ref, ohtl_ref, epd_ref, hid_ref, ed_ref,
    gg_ref, we_ref, ws_ref, wr_ref, node_ref, n0, n1, n2, n3, far_ref, cs_ref,
    ntot_ref, gat_ref, npd_ref, nhid_ref, nd_ref,
    ge_out, ntot_out, b0, b1, b2, b3, keep_out, give_out,
    dwe, dwo, csl, rs, g_in, g_out, v_in, v_out,
):
    step = pl.program_id(0)

    @pl.when(step == 0)
    def _():
        for ref in (dwe, dwo, csl, rs):
            ref[...] = jnp.zeros_like(ref)

    epd = epd_ref[...]
    total = cot_ref[...].astype(F32) + dot(ohr_ref[...], gg_ref[...])
    ge_out[...] = (total + dot_nt(epd, we_ref[...])).astype(BF)
    csl[...] += dot(ohtl_ref[...], epd)
    rs[...] += dot(ohrt_ref[...], epd)
    dwe[...] += dot_tn(edge_ref[...], epd)
    dwo[...] += dot_tn(hid_ref[...], ed_ref[...])

    @pl.when(step == steps - 1)
    def _():
        node = node_ref[...]
        rows = node.shape[0]
        width = n0.shape[0]
        loc = csl[:rows, :].astype(BF)
        near = csl[rows:, :].astype(BF)
        recv = rs[...].astype(BF)
        ws = ws_ref[...]
        ntot_out[...] = ntot_ref[...] + dot_nt(loc, ws) + dot_nt(recv, wr_ref[...])
        dws = dot_tn(node, loc) + dot_tn(far_ref[...], cs_ref[...])
        for k, (ref, back) in enumerate(zip((n0, n1, n2, n3), (b0, b1, b2, b3))):
            part = near[k * width : (k + 1) * width, :]
            back[...] = dot_nt(part, ws).astype(BF)
            dws = dws + dot_tn(ref[...], part)
        g_in[:D, :] = dwe[...].astype(BF)
        g_in[D : 2 * D, :] = dws.astype(BF)
        g_in[2 * D :, :] = dot_tn(node, recv).astype(BF)
        g_out[...] = dwo[...].astype(BF)
        npd = npd_ref[...]
        v_in[:D, :] = dot_tn(node, npd).astype(BF)
        v_in[D:, :] = dot_tn(gat_ref[...], npd).astype(BF)
        v_out[...] = dot_tn(nhid_ref[...], nd_ref[...]).astype(BF)

        me = core_ref[0]
        r = iota((256, 512), 0)
        q = iota((256, 512), 1)
        k = r // 32
        s = r % 32

        def picks(core):
            src = jnp.where(
                s < 12,
                24 * k + 12 * core + s,
                jnp.where(
                    s < 16,
                    192 + 8 * k + 4 * core + s - 12,
                    jnp.where(
                        s < 24,
                        256 + 16 * k + 8 * core + s - 16,
                        jnp.where(s < 28, 384 + 8 * k + 4 * core + s - 24, -1),
                    ),
                ),
            )
            return hot(src == q)

        mine = picks(me)
        other = picks(1 - me)
        for b in range(8):
            block = jnp.concatenate(
                [
                    g_in[192 * b : 192 * (b + 1), :],
                    g_out[64 * b : 64 * (b + 1), :],
                    v_in[128 * b : 128 * (b + 1), :],
                    v_out[64 * b : 64 * (b + 1), :],
                    jnp.zeros((64, D), BF),
                ],
                0,
            )
            keep_out[256 * b : 256 * (b + 1), :] = dot(mine, block).astype(BF)
            give_out[256 * b : 256 * (b + 1), :] = dot(other, block).astype(BF)


def owner_kernel(ntot_ref, near_ref, far_ref, b0, b1, b2, b3, back_ref, out):
    rows = ntot_ref.shape[0]
    total = ntot_ref[...]
    total = total + dot(hot(far_ref[...] == iota((rows, far_ref.shape[1]), 0)), back_ref[...])
    near = jnp.concatenate([b0[...], b1[...], b2[...], b3[...]], 0)
    total = total + dot(hot(near_ref[...] == iota((rows, near_ref.shape[1]), 0)), near)
    out[...] = total.astype(BF)


def sum_kernel(edge_scale, node_scale, got_ref, o0, o1, o2, o3):
    total = jnp.sum(got_ref[...].astype(F32), 0)
    o0[...] = total[0:12] * edge_scale
    o1[...] = total[12:16] * edge_scale
    o2[...] = total[16:24] * node_scale
    o3[...] = total[24:28] * node_scale


def shards(
    node_latent, edge_latent, node_cotangent, edge_cotangent,
    w_edge_in, w_edge_out, w_node_in, w_node_out,
    sender_code, receiver, near_list, far_list,
):
    rows, width = node_latent.shape
    edges = edge_latent.shape[0]
    n_row, n_col = lax.axis_size("row"), lax.axis_size("col")
    peers = n_row * n_col
    near_w = near_list.shape[2]
    far_w = far_list.shape[2]
    n_near, n_far = 4 * near_w, peers * far_w
    codes = rows + n_near + n_far
    tile = 512
    steps = edges // tile
    sds = jax.ShapeDtypeStruct

    near_send, far_send = pl.pallas_call(
        offer_kernel,
        out_shape=(sds((n_near, width), BF), sds((n_far, width), BF)),
        name="offer",
    )(node_latent, near_list, far_list)

    far = lax.all_to_all(far_send.reshape(peers, far_w, width), AXES, 0, 0, tiled=True)
    far = far.reshape(n_far, width)
    moves = (("row", 1), ("row", -1), ("col", 1), ("col", -1))

    def shifted(value, axis, by):
        n = lax.axis_size(axis)
        return lax.ppermute(value, axis, [(i, (i + by) % n) for i in range(n)])

    near = [
        shifted(near_send[k * near_w : (k + 1) * near_w], axis, by)
        for k, (axis, by) in enumerate(moves)
    ]

    code_c = sender_code.reshape(edges, 1)
    code_r = sender_code.reshape(1, edges)
    recv_c = receiver.reshape(edges, 1)
    recv_r = receiver.reshape(1, edges)

    def rowed(cols):
        return pl.BlockSpec((tile, cols), lambda s: (s, 0))

    def laned(lead):
        return pl.BlockSpec((lead, tile), lambda s: (0, s))

    def wpart(k):
        return pl.BlockSpec((width, width), lambda *_: (k, 0))

    pre_local, oh, oht, ohr, ohrt = pl.pallas_call(
        functools.partial(local_kernel, rows),
        grid=(steps,),
        in_specs=[
            rowed(width), full((rows, width)), wpart(0), wpart(1), wpart(2),
            rowed(1), laned(1), rowed(1), laned(1),
        ],
        out_specs=[rowed(width), rowed(codes - rows), laned(codes), rowed(rows), laned(rows)],
        out_shape=(
            sds((edges, width), F32),
            sds((edges, codes - rows), BF),
            sds((codes, edges), BF),
            sds((edges, rows), BF),
            sds((rows, edges), BF),
        ),
        scratch_shapes=[pltpu.VMEM((rows, width), BF), pltpu.VMEM((rows, width), BF)],
        compiler_params=params(),
        cost_estimate=cost(2 * edges * width * (width + 2 * rows), 22e6),
        name="local",
    )(edge_latent, node_latent, w_edge_in, w_edge_in, w_edge_in, code_c, code_r, recv_c, recv_r)

    def first(cols):
        return pl.BlockSpec((tile, cols), lambda s: (jnp.minimum(s, steps - 1), 0))

    def second(cols):
        return pl.BlockSpec((tile, cols), lambda s: (jnp.maximum(s - steps, 0), 0))

    near_spec = [full((near_w, width))] * 4
    node_spec = full((rows, width))
    sq = full((width, width))
    (
        edge_new, node_new, epd, hid, ed, gg, far_grad, cs_far, ntot, gat, npd, nhid, nd,
    ) = pl.pallas_call(
        functools.partial(main_kernel, steps),
        grid=(2 * steps,),
        in_specs=[
            first(width), first(codes - rows), first(width),
            pl.BlockSpec((rows, tile), lambda s: (0, jnp.minimum(s, steps - 1))),
            second(width), second(rows),
            pl.BlockSpec((pl.Element(n_far), pl.Element(tile)), lambda s: (rows + n_near, jnp.maximum(s - steps, 0) * tile)),
            *near_spec, full((n_far, width)), wpart(1), sq,
            node_spec, node_spec, wpart(0), wpart(1), sq,
        ],
        out_specs=[
            first(width), node_spec, second(width), full((edges, width)), second(width),
            node_spec, full((n_far, width)), full((n_far, width)), node_spec,
            node_spec, node_spec, node_spec, node_spec,
        ],
        out_shape=(
            sds((edges, width), BF), sds((rows, width), BF),
            sds((edges, width), BF), sds((edges, width), BF), sds((edges, width), BF),
            sds((rows, width), BF), sds((n_far, width), BF), sds((n_far, width), BF),
            sds((rows, width), F32),
            sds((rows, width), BF), sds((rows, width), BF),
            sds((rows, width), BF), sds((rows, width), BF),
        ),
        scratch_shapes=[
            pltpu.VMEM((codes - rows, width), BF),
            pltpu.VMEM((rows, width), F32),
            pltpu.VMEM((edges, width), BF),
            pltpu.VMEM((edges, width), BF),
            pltpu.VMEM((edges, 1), F32),
            pltpu.VMEM((n_far, width), F32),
        ],
        compiler_params=params(),
        cost_estimate=cost(14e9, 30e6),
        name="middle",
    )(
        pre_local, oh, edge_latent, ohrt, edge_cotangent, ohr, oht,
        *near, far, w_edge_in, w_edge_out,
        node_latent, node_cotangent, w_node_in, w_node_in, w_node_out,
    )

    far_back = lax.all_to_all(far_grad.reshape(peers, far_w, width), AXES, 0, 0, tiled=True)
    far_back = far_back.reshape(n_far, width)

    core = (lax.axis_index("col") % 2).astype(jnp.int32).reshape(1)
    out_rows = 32 * (peers // 2)
    rest = pl.pallas_call(
        functools.partial(rest_kernel, steps),
        grid=(steps,),
        in_specs=[
            pl.BlockSpec(memory_space=pltpu.SMEM),
            rowed(width), rowed(width), rowed(rows), laned(rows),
            pl.BlockSpec((rows + n_near, tile), lambda s: (0, s)),
            rowed(width), rowed(width), rowed(width),
            node_spec, wpart(0), wpart(1), wpart(2), node_spec, *near_spec,
            full((n_far, width)), full((n_far, width)),
            node_spec, node_spec, node_spec, node_spec, node_spec,
        ],
        out_specs=[
            rowed(width), node_spec, *near_spec,
            full((out_rows, width)), full((out_rows, width)),
        ],
        out_shape=(
            sds((edges, width), BF), sds((rows, width), F32),
            *[sds((near_w, width), BF)] * 4,
            sds((out_rows, width), BF), sds((out_rows, width), BF),
        ),
        scratch_shapes=[
            pltpu.VMEM((width, width), F32), pltpu.VMEM((width, width), F32),
            pltpu.VMEM((rows + n_near, width), F32), pltpu.VMEM((rows, width), F32),
            pltpu.VMEM((3 * width, width), BF), pltpu.VMEM((width, width), BF),
            pltpu.VMEM((2 * width, width), BF), pltpu.VMEM((width, width), BF),
        ],
        compiler_params=params(),
        cost_estimate=cost(9e9, 24e6),
        name="rest",
    )
    grad_edge, ntot2, b0, b1, b2, b3, keep, give = rest(
        core, edge_latent, edge_cotangent, ohr, ohrt, oht, epd, hid, ed, gg,
        w_edge_in, w_edge_in, w_edge_in, node_latent, *near, far, cs_far,
        ntot, gat, npd, nhid, nd,
    )

    got = lax.ppermute(give, "col", [(i, i ^ 1) for i in range(n_col)])
    pair = (keep.astype(F32) + got.astype(F32)).astype(BF).reshape(peers // 2, 32, width)
    same_core = [[2 * i + c for i in range(peers // 2)] for c in range(2)]
    parts = lax.all_to_all(pair, AXES, 0, 0, axis_index_groups=same_core, tiled=True)

    back = [shifted(b, axis, -by) for b, (axis, by) in zip((b0, b1, b2, b3), moves)]
    grad_node = pl.pallas_call(
        owner_kernel,
        out_shape=sds((rows, width), BF),
        name="owner",
        cost_estimate=cost(4e8, 3e6),
    )(ntot2, near_list.reshape(1, n_near), far_list.reshape(1, n_far), *back, far_back)

    edge_scale = 1.0 / math.sqrt(edges * peers)
    node_scale = 1.0 / math.sqrt(rows * peers)
    g0, g1, g2, g3 = pl.pallas_call(
        functools.partial(sum_kernel, edge_scale, node_scale),
        out_shape=(
            sds((12, width), F32), sds((4, width), F32),
            sds((8, width), F32), sds((4, width), F32),
        ),
        name="total",
    )(parts)
    return (node_new, edge_new, grad_node, grad_edge, g0, g1, g2, g3)


def solution(mesh):
    both = P(AXES, None)
    in_specs = (
        both, both, both, both, P(), P(), P(), P(), P(AXES), P(AXES),
        P(AXES, None, None), P(AXES, None, None),
    )
    return jax.shard_map(
        shards, mesh=mesh, in_specs=in_specs, out_specs=(both,) * 8, check_vma=False
    )
```

time: 290 us -> 154 us (0.53)
  local copies, waits for them, and re-layouts: 97.7 us -> 9.46 us
  Pallas kernels: 0 us -> 63.2 us
  matrix products: 55 us -> 0 us
  starting transfers between devices: 56.2 us -> 39.6 us
  other arithmetic: 19.5 us -> 3.54 us
  between operations: 14.9 us -> 0.85 us
  waiting for transfers between devices: 41.6 us -> 35 us
    pallas_call x0 -> x6, Pallas kernels: none -> 63.2 us  [the longest x1 25.4 us: shards(): pl.pallas_call(functools.partial(main_kernel, steps), grid=(2 * steps,),...]
    dot_general x23 -> x0, matrix products: 55 us -> none  [the longest x8 16.2 us: plain_dot(): return jnp.dot(left, right, preferred_element_type=jnp.float32)]
    gather x8 -> x0, local copies, waits for them, and re-layouts: 47.1 us -> none  [the longest x2 14.5 us: shards(): jnp.take(gathered_grad, receiver, axis=0)]
    reduce_scatter x3 -> x0, waiting for transfers between devices: 23.5 us -> none  [shards(): lax.psum_scatter(shortened(shaped), 'col', scatter_dimension=1, tiled=True)]
    convert_element_type x7 -> x0, local copies, waits for them, and re-layouts: 18 us -> none  [the longest x6 15.6 us: shortened(): a.astype(jnp.bfloat16)]
    unnamed x81 -> x39, local copies, waits for them, and re-layouts: 20.8 us -> 5.42 us
    ppermute x8 -> x9, waiting for transfers between devices: 5.05 us -> 16.9 us  [the longest x8 16.9 us: shifted(): return lax.ppermute(value, axis, [(i, (i + by) % n) for i in range(n)])]
    all_to_all x6 -> x3, starting transfers between devices: 37.3 us -> 25.5 us  [the longest x1 11.2 us: shards(): lax.all_to_all(far_send.reshape(peers, far_w, width), AXES, 0, 0, tiled=T...]
  transfers between devices with their start and end apart: 18 -> 12, of which waited for: 6 -> 6; matrix products, arithmetic and copies ran while one was open for 45% -> 5% of each run, Pallas kernels for 0% -> 9%
where the time goes in v1:
time: 154 us; the launch traced here: 152 us
  Pallas kernels  63.2 us (41%)
  starting transfers between devices  39.6 us (26%)
  waiting for transfers between devices  35 us (23%)
  local copies, waits for them, and re-layouts  9.46 us (6%)
  other arithmetic  3.54 us (2%)
    pallas_call x1, Pallas kernels, shards(): pl.pallas_call(functools.partial(main_kernel, steps), grid=(2 * steps,),...  25.4 us
    pallas_call x1, Pallas kernels, shards(): rest(core, edge_latent, edge_cotangent, ohr, ohrt, oht, epd, hid, ed, gg,...  19 us
    ppermute x8, waiting for transfers between devices, shifted(): return lax.ppermute(value, axis, [(i, (i + by) % n) for i in range(n)])  16.9 us
    all_to_all x1, waiting for transfers between devices, shards(): lax.all_to_all(far_grad.reshape(peers, far_w, width), AXES, 0, 0, tiled=T...  15.6 us
    ppermute x8, starting transfers between devices, shifted(): return lax.ppermute(value, axis, [(i, (i + by) % n) for i in range(n)])  14 us
    all_to_all x1, starting transfers between devices, shards(): lax.all_to_all(far_send.reshape(peers, far_w, width), AXES, 0, 0, tiled=T...  11.2 us
    pallas_call x1, Pallas kernels, shards(): pl.pallas_call(functools.partial(local_kernel, rows), grid=(steps,), in_s...  10.9 us
    all_to_all x1, starting transfers between devices, shards(): lax.all_to_all(far_grad.reshape(peers, far_w, width), AXES, 0, 0, tiled=T...  9.49 us
  transfers between devices with their start and end apart: 12, of which 6 were waited for; matrix products, arithmetic and copies ran while one was open for 5% of the time, Pallas kernels for 9%

profile of v1, /device:TPU:0, one launch (start us, length us, event | category | flops | bytes accessed | tf_op | source)
XLA Modules:
  0.0 151.6 jit_solution(18181362132108215892)
XLA Ops:
  0.7 1.4 copy.24.far_ref
  2.1 2.7 %offer.1 = (bf16[256,512]{1,0:T(8,128)(2,1)}, bf16[1024,512]{1,0:T(8,128)(2,1)}) custom-call(bf16[256,512]{1,0:T(8,128)(2,1)} %node_ref.7, s32[1,4,64]{2,1,0:T(4,128)} %near_ref.1, s32[1,128,8]{2,1,0:T(8,128)} %copy.24.far_ref), custom_call_target="tpu_custom_call" | custom-call | tf_op jit(solution)/shard_map/offer/pallas_call | solution.py:304
  4.7 11.2 %all-to-all-start = ((bf16[128,8,512]{2,1,0:T(8,128)(2,1)}), bf16[128,8,512]{2,1,0:T(8,128)(2,1)S(1)}, u32[]{:S(2)}, u32[]{:S(2)}) async-start(bf16[128,8,512]{2,1,0:T(8,128)(2,1)} %bitcast.13), calls=%async_computation | async-start | bytes 2097152 | tf_op jit(solution)/shard_map/all_to_all | solution.py:310
  16.0 1.9 %collective-permute-start.3 = (bf16[64,512]{1,0:T(8,128)(2,1)S(1)}, bf16[64,512]{1,0:T(8,128)(2,1)S(1)}, u32[]{:S(2)}, u32[]{:S(2)}) collective-permute-start(bf16[64,512]{1,0:T(8,128)(2,1)S(1)} %get-tuple-element.72), channel_id=1, source_target_pairs={{0,7},{1,0},{2,1},{3,2},{4,3},{5,4},{6,5},{7,6},{8,15},{9,8},{10,9... | collective-permute-start | bytes 196616 | tf_op jit(solution)/shard_map/ppermute | solution.py:316
  17.9 5.7 %collective-permute-start.1 = (bf16[64,512]{1,0:T(8,128)(2,1)S(1)}, bf16[64,512]{1,0:T(8,128)(2,1)S(1)}, u32[]{:S(2)}, u32[]{:S(2)}) collective-permute-start(bf16[64,512]{1,0:T(8,128)(2,1)S(1)} %get-tuple-element.74), channel_id=1, source_target_pairs={{0,120},{8,0},{16,8},{24,16},{32,24},{40,32},{48,40},{56,48},{64,5... | collective-permute-start | bytes 196616 | tf_op jit(solution)/shard_map/ppermute | solution.py:316
  23.6 1.3 copy.23.recv_c
  24.9 1.3 copy.22.code_c
  26.3 10.9 %local.1 = (f32[2048,512]{1,0:T(8,128)}, bf16[2048,1280]{1,0:T(8,128)(2,1)}, bf16[1536,2048]{1,0:T(8,128)(2,1)}, bf16[2048,256]{1,0:T(8,128)(2,1)}, bf16[256,2048]{1,0:T(8,128)(2,1)}) custom-call(bf16[2048,512]{1,0:T(8,128)(2,1)} %edge_ref.5, bf16[256,512]{1,0:T(8,128)(2,1)} %node_ref.7, bf16[1536,512]{1,0:T(8,128)(2,1)} %wr_ref.3, ...), custom_call_target="tpu_custom_call" | custom-call | flops 2147483648 | bytes 22000000 | tf_op jit(solution)/shard_map/local/pallas_call | solution.py:337
  38.3 25.4 %middle.1 = (bf16[2048,512]{1,0:T(8,128)(2,1)}, bf16[256,512]{1,0:T(8,128)(2,1)}, bf16[2048,512]{1,0:T(8,128)(2,1)}, bf16[2048,512]{1,0:T(8,128)(2,1)}, bf16[204...) custom-call(f32[2048,512]{1,0:T(8,128)} %get-tuple-element.40.p_ref,, ...), custom_call_target="tpu_custom_call" | custom-call | flops 14000000000 | bytes 30000000 | tf_op jit(solution)/shard_map/middle/pallas_call | solution.py:369
  63.7 19.0 %rest.1 = (bf16[2048,512]{1,0:T(8,128)(2,1)}, f32[256,512]{1,0:T(8,128)}, bf16[64,512]{1,0:T(8,128)(2,1)}, bf16[64,512]{1,0:T(8,128)(2,1)}, bf16[64,512]{1,0:T(8...) custom-call(s32[1]{0:T(128)} %bitcast.6.core_ref, ...), custom_call_target="tpu_custom_call" | custom-call | flops 8999999488 | bytes 24000000 | tf_op jit(solution)/shard_map/rest/pallas_call | solution.py:446
  82.8 9.5 %all-to-all-start.1 = ((bf16[128,8,512]{2,1,0:T(8,128)(2,1)}), bf16[128,8,512]{2,1,0:T(8,128)(2,1)S(1)}, u32[]{:S(2)}, u32[]{:S(2)}) async-start(bf16[128,8,512]{2,1,0:T(8,128)(2,1)} %bitcast.14), calls=%async_computation.1 | async-start | bytes 2097152 | tf_op jit(solution)/shard_map/all_to_all | solution.py:410
  92.3 3.5 %add_convert_fusion = bf16[2048,512]{1,0:T(8,128)(2,1)} fusion(bf16[2048,512]{1,0:T(8,128)(2,1)} %collective-permute-done.8, bf16[2048,512]{1,0:T(8,128)(2,1)S(1)} %copy-done.2), kind=kLoop, calls=%fused_computation | loop fusion | flops 4194304 | bytes 6291456 | tf_op jit(solution)/shard_map/convert_element_type | solution.py:453
  95.8 15.6 %all-to-all-done.1 = bf16[128,8,512]{2,1,0:T(8,128)(2,1)S(1)} async-done(((bf16[128,8,512]{2,1,0:T(8,128)(2,1)}), bf16[128,8,512]{2,1,0:T(8,128)(2,1)S(1)}, u32[]{:S(2)}, u32[]{:S(2)}) %all-to-all-start.1) | async-done | bytes 1048608 | tf_op jit(solution)/shard_map/all_to_all | solution.py:410
  112.4 4.9 %all-to-all-start.2 = ((bf16[64,32,512]{2,1,0:T(8,128)(2,1)}), bf16[64,32,512]{2,1,0:T(8,128)(2,1)S(1)}, u32[]{:S(2)}, u32[]{:S(2)}) async-start(bf16[64,32,512]{2,1,0:T(8,128)(2,1)} %bitcast.9), calls=%async_computation.2 | async-start | bytes 4194304 | tf_op jit(solution)/shard_map/all_to_all | solution.py:455
  117.3 5.3 %collective-permute-start.4 = (bf16[64,512]{1,0:T(8,128)(2,1)}, bf16[64,512]{1,0:T(8,128)(2,1)S(1)}, u32[]{:S(2)}, u32[]{:S(2)}) collective-permute-start(bf16[64,512]{1,0:T(8,128)(2,1)} %get-tuple-element.60), channel_id=1, source_target_pairs={{0,120},{8,0},{16,8},{24,16},{32,24},{40,32},{48,40},{56,48},{64,5... | collective-permute-start | bytes 196616 | tf_op jit(solution)/shard_map/ppermute | solution.py:316
  122.5 1.1 collective-permute-start.6
  124.9 10.7 %collective-permute-done.4.b0 = bf16[64,512]{1,0:T(8,128)(2,1)S(1)} collective-permute-done((bf16[64,512]{1,0:T(8,128)(2,1)}, bf16[64,512]{1,0:T(8,128)(2,1)S(1)}, u32[]{:S(2)}, u32[]{:S(2)}) %collective-permute-start.4) | collective-permute-done | bytes 65568 | tf_op jit(solution)/shard_map/ppermute | solution.py:316
  135.6 1.6 %collective-permute-done.5.b1 = bf16[64,512]{1,0:T(8,128)(2,1)S(1)} collective-permute-done((bf16[64,512]{1,0:T(8,128)(2,1)}, bf16[64,512]{1,0:T(8,128)(2,1)S(1)}, u32[]{:S(2)}, u32[]{:S(2)}) %collective-permute-start.5) | collective-permute-done | bytes 65568 | tf_op jit(solution)/shard_map/ppermute | solution.py:316
  137.3 2.7 %collective-permute-done.6.b2 = bf16[64,512]{1,0:T(8,128)(2,1)S(1)} collective-permute-done((bf16[64,512]{1,0:T(8,128)(2,1)S(1)}, bf16[64,512]{1,0:T(8,128)(2,1)S(1)}, u32[]{:S(2)}, u32[]{:S(2)}) %collective-permute-start.6) | collective-permute-done | bytes 65568 | tf_op jit(solution)/shard_map/ppermute | solution.py:316
  139.9 1.9 %collective-permute-done.7.b3 = bf16[64,512]{1,0:T(8,128)(2,1)S(1)} collective-permute-done((bf16[64,512]{1,0:T(8,128)(2,1)S(1)}, bf16[64,512]{1,0:T(8,128)(2,1)S(1)}, u32[]{:S(2)}, u32[]{:S(2)}) %collective-permute-start.7) | collective-permute-done | bytes 65568 | tf_op jit(solution)/shard_map/ppermute | solution.py:316
  142.5 2.7 %owner.1 = bf16[256,512]{1,0:T(8,128)(2,1)} custom-call(f32[256,512]{1,0:T(8,128)} %get-tuple-element.59.ntot_ref, s32[1,256]{1,0:T(1,128)} %reshape.59.near_ref, s32[1,1024]{1,0:T(1,128)} %reshape.60.far_ref, bf16[64,512]{1,0:T(8,128)(2,1)} %copy-done.6, bf16[64,512]{1,0:T(8,128)(2,1)} %copy-done.7, bf16[64,512]{1,0:T(8,128)(2,1)} %copy-done.8, ...), custom_call_target="tpu_custom_call" | custom-call | flops 400000000 | bytes 3000000 | tf_op jit(solution)/shard_map/owner/pallas_call | solution.py:458
  145.2 2.5 %all-to-all-done.2.got_ref = bf16[64,32,512]{2,1,0:T(8,128)(2,1)S(1)} async-done(((bf16[64,32,512]{2,1,0:T(8,128)(2,1)}), bf16[64,32,512]{2,1,0:T(8,128)(2,1)S(1)}, u32[]{:S(2)}, u32[]{:S(2)}) %all-to-all-start.2) | async-done | bytes 2097184 | tf_op jit(solution)/shard_map/all_to_all | solution.py:455
  147.8 1.4 copy-done
  149.1 2.5 %total.1 = (f32[12,512]{1,0:T(8,128)}, f32[4,512]{1,0:T(4,128)}, f32[8,512]{1,0:T(8,128)}, f32[4,512]{1,0:T(4,128)}) custom-call(bf16[64,32,512]{2,1,0:T(8,128)(2,1)} %copy-done), custom_call_target="tpu_custom_call" | custom-call | tf_op jit(solution)/shard_map/total/pallas_call | solution.py:467
  (51 shorter events, 4.1 us)
Async XLA Ops:
  0.6 22.9 %copy-start.11 = (s32[2048]{0:T(1024)S(1)}, s32[2048]{0:T(1024)}, u32[]{:S(2)}) copy-start(s32[2048]{0:T(1024)} %param.21) | copy-start | bytes 24580
  0.6 24.3 %copy-start.10 = (s32[2048]{0:T(1024)S(1)}, s32[2048]{0:T(1024)}, u32[]{:S(2)}) copy-start(s32[2048]{0:T(1024)} %param.20) | copy-start | bytes 24580
  4.7 11.2 %copy-start.5 = (bf16[256,512]{1,0:T(8,128)(2,1)S(1)}, bf16[256,512]{1,0:T(8,128)(2,1)}, u32[]{:S(2)}) copy-start(bf16[256,512]{1,0:T(8,128)(2,1)} %get-tuple-element.45) | copy-start | bytes 786436
  4.7 32.5 %all-to-all-start = ((bf16[128,8,512]{2,1,0:T(8,128)(2,1)}), bf16[128,8,512]{2,1,0:T(8,128)(2,1)S(1)}, u32[]{:S(2)}, u32[]{:S(2)}) async-start(bf16[128,8,512]{2,1,0:T(8,128)(2,1)} %bitcast.13), calls=%async_computation | async-start | bytes 2097152 | tf_op jit(solution)/shard_map/all_to_all | solution.py:310
  16.0 21.2 %collective-permute-start.3 = (bf16[64,512]{1,0:T(8,128)(2,1)S(1)}, bf16[64,512]{1,0:T(8,128)(2,1)S(1)}, u32[]{:S(2)}, u32[]{:S(2)}) collective-permute-start(bf16[64,512]{1,0:T(8,128)(2,1)S(1)} %get-tuple-element.72), channel_id=1, source_target_pairs={{0,7},{1,0},{2,1},{3,2},{4,3},{5,4},{6,5},{7,6},{8,15},{9,8},{10,9... | collective-permute-start | bytes 196616 | tf_op jit(solution)/shard_map/ppermute | solution.py:316
  17.9 19.3 %collective-permute-start.2 = (bf16[64,512]{1,0:T(8,128)(2,1)S(1)}, bf16[64,512]{1,0:T(8,128)(2,1)S(1)}, u32[]{:S(2)}, u32[]{:S(2)}) collective-permute-start(bf16[64,512]{1,0:T(8,128)(2,1)S(1)} %get-tuple-element.73), channel_id=1, source_target_pairs={{0,1},{1,2},{2,3},{3,4},{4,5},{5,6},{6,7},{7,0},{8,9},{9,10},{10,1... | collective-permute-start | bytes 196616 | tf_op jit(solution)/shard_map/ppermute | solution.py:316
  17.9 19.3 %collective-permute-start.1 = (bf16[64,512]{1,0:T(8,128)(2,1)S(1)}, bf16[64,512]{1,0:T(8,128)(2,1)S(1)}, u32[]{:S(2)}, u32[]{:S(2)}) collective-permute-start(bf16[64,512]{1,0:T(8,128)(2,1)S(1)} %get-tuple-element.74), channel_id=1, source_target_pairs={{0,120},{8,0},{16,8},{24,16},{32,24},{40,32},{48,40},{56,48},{64,5... | collective-permute-start | bytes 196616 | tf_op jit(solution)/shard_map/ppermute | solution.py:316
  23.6 13.7 %collective-permute-start = (bf16[64,512]{1,0:T(8,128)(2,1)S(1)}, bf16[64,512]{1,0:T(8,128)(2,1)S(1)}, u32[]{:S(2)}, u32[]{:S(2)}) collective-permute-start(bf16[64,512]{1,0:T(8,128)(2,1)S(1)} %get-tuple-element.75), channel_id=1, source_target_pairs={{0,8},{8,16},{16,24},{24,32},{32,40},{40,48},{48,56},{56,64},{64,7... | collective-permute-start | bytes 196616 | tf_op jit(solution)/shard_map/ppermute | solution.py:316
  82.7 9.6 %copy-start.2 = (bf16[2048,512]{1,0:T(8,128)(2,1)S(1)}, bf16[2048,512]{1,0:T(8,128)(2,1)}, u32[]{:S(2)}) copy-start(bf16[2048,512]{1,0:T(8,128)(2,1)} %get-tuple-element.66) | copy-start | bytes 6291460
  82.7 9.6 %collective-permute-start.8 = (bf16[2048,512]{1,0:T(8,128)(2,1)}, bf16[2048,512]{1,0:T(8,128)(2,1)}, u32[]{:S(2)}, u32[]{:S(2)}) collective-permute-start(bf16[2048,512]{1,0:T(8,128)(2,1)} %get-tuple-element.67), channel_id=1, source_target_pairs={{0,1},{1,0},{2,3},{3,2},{4,5},{5,4},{6,7},{7,6},{8,9},{9,8},{10,11... | collective-permute-start | bytes 6291464 | tf_op jit(solution)/shard_map/ppermute | solution.py:452
  82.8 28.6 %all-to-all-start.1 = ((bf16[128,8,512]{2,1,0:T(8,128)(2,1)}), bf16[128,8,512]{2,1,0:T(8,128)(2,1)S(1)}, u32[]{:S(2)}, u32[]{:S(2)}) async-start(bf16[128,8,512]{2,1,0:T(8,128)(2,1)} %bitcast.14), calls=%async_computation.1 | async-start | bytes 2097152 | tf_op jit(solution)/shard_map/all_to_all | solution.py:410
  111.4 11.1 %copy-start.18 = (bf16[64,512]{1,0:T(8,128)(2,1)S(1)}, bf16[64,512]{1,0:T(8,128)(2,1)}, u32[]{:S(2)}) copy-start(bf16[64,512]{1,0:T(8,128)(2,1)} %get-tuple-element.62) | copy-start | bytes 196612
  111.4 12.2 %copy-start.17 = (bf16[64,512]{1,0:T(8,128)(2,1)S(1)}, bf16[64,512]{1,0:T(8,128)(2,1)}, u32[]{:S(2)}) copy-start(bf16[64,512]{1,0:T(8,128)(2,1)} %get-tuple-element.63) | copy-start | bytes 196612
  111.4 12.2 %copy-start.12 = (s32[1,4,64]{2,1,0:T(4,128)S(1)}, s32[1,4,64]{2,1,0:T(4,128)}, u32[]{:S(2)}) copy-start(s32[1,4,64]{2,1,0:T(4,128)} %near_ref.1) | copy-start | bytes 3076
  111.4 12.9 %copy-start.4 = (s32[1,128,8]{2,1,0:T(8,128)S(1)}, s32[1,128,8]{2,1,0:T(8,128)}, u32[]{:S(2)}) copy-start(s32[1,128,8]{2,1,0:T(8,128)} %copy.24.far_ref) | copy-start | bytes 12292
  112.4 35.4 %all-to-all-start.2 = ((bf16[64,32,512]{2,1,0:T(8,128)(2,1)}), bf16[64,32,512]{2,1,0:T(8,128)(2,1)S(1)}, u32[]{:S(2)}, u32[]{:S(2)}) async-start(bf16[64,32,512]{2,1,0:T(8,128)(2,1)} %bitcast.9), calls=%async_computation.2 | async-start | bytes 4194304 | tf_op jit(solution)/shard_map/all_to_all | solution.py:455
  117.3 18.4 %collective-permute-start.4 = (bf16[64,512]{1,0:T(8,128)(2,1)}, bf16[64,512]{1,0:T(8,128)(2,1)S(1)}, u32[]{:S(2)}, u32[]{:S(2)}) collective-permute-start(bf16[64,512]{1,0:T(8,128)(2,1)} %get-tuple-element.60), channel_id=1, source_target_pairs={{0,120},{8,0},{16,8},{24,16},{32,24},{40,32},{48,40},{56,48},{64,5... | collective-permute-start | bytes 196616 | tf_op jit(solution)/shard_map/ppermute | solution.py:316
  122.5 14.7 %collective-permute-start.5 = (bf16[64,512]{1,0:T(8,128)(2,1)}, bf16[64,512]{1,0:T(8,128)(2,1)S(1)}, u32[]{:S(2)}, u32[]{:S(2)}) collective-permute-start(bf16[64,512]{1,0:T(8,128)(2,1)} %get-tuple-element.61), channel_id=1, source_target_pairs={{0,8},{8,16},{16,24},{24,32},{32,40},{40,48},{48,56},{56,64},{64,7... | collective-permute-start | bytes 196616 | tf_op jit(solution)/shard_map/ppermute | solution.py:316
  122.5 17.4 %collective-permute-start.6 = (bf16[64,512]{1,0:T(8,128)(2,1)S(1)}, bf16[64,512]{1,0:T(8,128)(2,1)S(1)}, u32[]{:S(2)}, u32[]{:S(2)}) collective-permute-start(bf16[64,512]{1,0:T(8,128)(2,1)S(1)} %copy-done.18), channel_id=1, source_target_pairs={{0,7},{1,0},{2,1},{3,2},{4,3},{5,4},{6,5},{7,6},{8,15},{9,8},{10,9... | collective-permute-start | bytes 196616 | tf_op jit(solution)/shard_map/ppermute | solution.py:316
  123.6 18.3 %collective-permute-start.7 = (bf16[64,512]{1,0:T(8,128)(2,1)S(1)}, bf16[64,512]{1,0:T(8,128)(2,1)S(1)}, u32[]{:S(2)}, u32[]{:S(2)}) collective-permute-start(bf16[64,512]{1,0:T(8,128)(2,1)S(1)} %copy-done.17), channel_id=1, source_target_pairs={{0,1},{1,2},{2,3},{3,4},{4,5},{5,6},{6,7},{7,0},{8,9},{9,10},{10,1... | collective-permute-start | bytes 196616 | tf_op jit(solution)/shard_map/ppermute | solution.py:316
  135.6 6.3 %copy-start.6 = (bf16[64,512]{1,0:T(8,128)(2,1)}, bf16[64,512]{1,0:T(8,128)(2,1)S(1)}, u32[]{:S(2)}) copy-start(bf16[64,512]{1,0:T(8,128)(2,1)S(1)} %collective-permute-done.4.b0) | copy-start | bytes 196612
  137.3 4.6 %copy-start.7 = (bf16[64,512]{1,0:T(8,128)(2,1)}, bf16[64,512]{1,0:T(8,128)(2,1)S(1)}, u32[]{:S(2)}) copy-start(bf16[64,512]{1,0:T(8,128)(2,1)S(1)} %collective-permute-done.5.b1) | copy-start | bytes 196612
  139.9 1.9 %copy-start.8 = (bf16[64,512]{1,0:T(8,128)(2,1)}, bf16[64,512]{1,0:T(8,128)(2,1)S(1)}, u32[]{:S(2)}) copy-start(bf16[64,512]{1,0:T(8,128)(2,1)S(1)} %collective-permute-done.6.b2) | copy-start | bytes 196612
  147.8 1.4 copy-start
  (7 other events, 5.2 us)

commit v2 on v1

v2 whole, which is shorter than its diff:
```python
import functools
import math

import jax
import jax.numpy as jnp
from jax import lax
from jax.experimental import pallas as pl
from jax.experimental.pallas import tpu as pltpu
from jax.sharding import PartitionSpec as P


EPS = 1e-05
BF = jnp.bfloat16
F32 = jnp.float32
AXES = ("row", "col")
D = 512
EG = 1024
NG = 384
TILE = 512
SUB = 128
VMEM_LIMIT = 67043328


def dot(left, right):
    return jnp.dot(left, right, preferred_element_type=F32)


def dot_nt(left, right):
    return lax.dot_general(left, right, (((1,), (1,)), ((), ())), preferred_element_type=F32)


def dot_tn(left, right):
    return lax.dot_general(left, right, (((0,), (0,)), ((), ())), preferred_element_type=F32)


def iota(shape, dim):
    return lax.broadcasted_iota(jnp.int32, shape, dim)


def hot(mask):
    return jnp.where(mask, 1.0, 0.0).astype(BF)


def normed(value):
    mean = jnp.mean(value, -1, keepdims=True)
    centred = value - mean
    recip = lax.rsqrt(jnp.mean(centred * centred, -1, keepdims=True) + EPS)
    return centred * recip, recip


def norm_grad(y, recip, grad):
    inner = grad - jnp.mean(grad, -1, keepdims=True) - y * jnp.mean(grad * y, -1, keepdims=True)
    return recip * inner


def full(shape):
    return pl.BlockSpec(shape, lambda *_: (0,) * len(shape))


def params(axes=1):
    return pltpu.CompilerParams(
        dimension_semantics=("arbitrary",) * axes, vmem_limit_bytes=VMEM_LIMIT
    )


def cost(flops, nbytes):
    return pl.CostEstimate(flops=int(flops), bytes_accessed=int(nbytes), transcendentals=0)


def column_of(table_t, groups, width):
    rows = groups * width
    pick = hot(iota((rows, groups), 0) // width == iota((rows, groups), 1))
    spread = dot_nt(pick, table_t.astype(F32).astype(BF))
    keep = iota((rows, width), 0) % width == iota((rows, width), 1)
    return jnp.sum(jnp.where(keep, spread, 0.0), -1, keepdims=True).astype(jnp.int32)


def lanes_to_rows(blocks, count, first):
    pick = hot(iota((count, blocks.shape[0]), 0) // 128 + first == iota((count, blocks.shape[0]), 1))
    spread = dot(pick, blocks.astype(F32).astype(BF))
    keep = iota((count, 128), 0) % 128 == iota((count, 128), 1)
    return jnp.sum(jnp.where(keep, spread, 0.0), -1, keepdims=True).astype(jnp.int32)


def row_of(table_t, count, group_of):
    width, groups = table_t.shape
    pick = hot(iota((groups, count), 0) == group_of(iota((groups, count), 1) // width))
    spread = dot(table_t.astype(F32).astype(BF), pick)
    keep = iota((width, count), 1) % width == iota((width, count), 0)
    return jnp.sum(jnp.where(keep, spread, 0.0), 0, keepdims=True).astype(jnp.int32)


def offer_kernel(node_ref, near_ref, far_ref, n0, n1, n2, n3, far_out):
    node = node_ref[...]
    rows = node.shape[0]
    far_col = column_of(far_ref[...], far_ref.shape[1], far_ref.shape[0])
    far_out[...] = dot(hot(far_col == iota((far_col.shape[0], rows), 1)), node).astype(BF)
    near = near_ref[0]
    for k, out in enumerate((n0, n1, n2, n3)):
        pick = hot(near[k : k + 1, :] == iota((rows, near.shape[1]), 0))
        out[...] = dot_tn(pick, node).astype(BF)


def local_kernel(
    rows, edge_ref, node_ref, we_ref, ws_ref, wr_ref, code_b, code_r, recv_b, recv_r,
    p_out, oh_out, oht_out, ohr_out, ohrt_out, nwr, nws,
):
    @pl.when(pl.program_id(0) == 0)
    def _():
        node = node_ref[...]
        nwr[...] = dot(node, wr_ref[...]).astype(BF)
        nws[...] = dot(node, ws_ref[...]).astype(BF)

    tile = edge_ref.shape[0]
    first = pl.program_id(0) * (tile // 128)
    code = 256 * lanes_to_rows(code_b[...] // 256, tile, first)
    code = code + lanes_to_rows(code_b[...] % 256, tile, first)
    ohr = hot(lanes_to_rows(recv_b[...], tile, first) == iota((tile, rows), 1))
    ohl = hot(code == iota((tile, rows), 1))
    p_out[...] = dot(edge_ref[...], we_ref[...]) + dot(ohr, nwr[...]) + dot(ohl, nws[...])
    ohr_out[...] = ohr
    oh_out[...] = hot(code - rows == iota(oh_out.shape, 1))
    oht_out[...] = hot(code_r[...] == iota(oht_out.shape, 0))
    ohrt_out[...] = hot(recv_r[...] == iota(ohrt_out.shape, 0))


def forward_kernel(
    steps, sub, core_ref,
    p_ref, oh_ref, edge_ref, ohrt_ref,
    n0, n1, n2, n3, far_ref, ws_ref, wo_ref,
    node_ref, ncot_ref, va_ref, vb_ref, vo_ref,
    enew_out, y_out, sp_out, hid_out, rec_out,
    nnew_out, gg_out, ntot_out, keep_out, give_out,
    tws, acc, v_in, v_out,
):
    step = pl.program_id(0)
    tile = edge_ref.shape[0]
    width = n0.shape[0]

    @pl.when(step == 0)
    def _():
        ws = ws_ref[...]
        for k, ref in enumerate((n0, n1, n2, n3)):
            tws[k * width : (k + 1) * width, :] = dot(ref[...], ws).astype(BF)
        tws[4 * width :, :] = dot(far_ref[...], ws).astype(BF)
        acc[...] = jnp.zeros_like(acc)

    for lo in range(0, tile, sub):
        here = slice(lo, lo + sub)
        pre = p_ref[here, :] + dot(oh_ref[here, :], tws[...])
        sigma = jax.nn.sigmoid(pre)
        hidden = pre * sigma
        hid = hidden.astype(BF)
        hid_out[here, :] = hid
        sp_out[here, :] = (sigma + hidden * (1.0 - sigma)).astype(BF)
        mid = dot(hid, wo_ref[...])
        y, rec = normed(mid)
        y_out[here, :] = y.astype(BF)
        rec_out[here, :] = rec
        enew_out[here, :] = (edge_ref[here, :].astype(F32) + y).astype(BF)
    acc[...] += dot(ohrt_ref[...], enew_out[...])

    @pl.when(step == steps - 1)
    def _():
        node = node_ref[...]
        gat = acc[...].astype(BF)
        pre = dot(node, va_ref[...]) + dot(gat, vb_ref[...])
        sigma = jax.nn.sigmoid(pre)
        hidden = pre * sigma
        hid = hidden.astype(BF)
        mid = dot(hid, vo_ref[...])
        y, rec = normed(mid)
        nnew_out[...] = (node.astype(F32) + y).astype(BF)
        ncot = ncot_ref[...].astype(F32)
        nd = norm_grad(y, rec, ncot).astype(BF)
        npd = (dot_nt(nd, vo_ref[...]) * (sigma + hidden * (1.0 - sigma))).astype(BF)
        gg_out[...] = dot_nt(npd, vb_ref[...]).astype(BF)
        ntot_out[...] = ncot + dot_nt(npd, va_ref[...])
        v_in[:D, :] = dot_tn(node, npd).astype(BF)
        v_in[D:, :] = dot_tn(gat, npd).astype(BF)
        v_out[...] = dot_tn(hid, nd).astype(BF)
        pack_nodes(core_ref[0], v_in, v_out, keep_out, give_out)


def pack_nodes(me, v_in, v_out, keep_out, give_out):
    r = iota((128, 256), 0)
    q = iota((128, 256), 1)
    k, s = r // 8, r % 8
    whole = hot(8 * k + s == q)
    split = 128 + 4 * k + s % 4 == q
    low = hot(split & (s < 4))
    high = hot(split & (s >= 4))
    half, quarter = D // 2, D // 4
    for b in range(8):
        node = jnp.concatenate(
            [
                v_in[128 * b : 128 * (b + 1), :],
                v_out[64 * b : 64 * (b + 1), :],
                jnp.zeros((64, D), BF),
            ],
            0,
        )
        w = dot(whole, node)
        lo = dot(low, node)
        hi = dot(high, node)
        at = slice(128 * b, 128 * (b + 1))
        parts = [
            (
                w[:, half * h : half * (h + 1)],
                lo[:, half * h : half * h + quarter] + hi[:, half * h + quarter : half * (h + 1)],
            )
            for h in range(2)
        ]
        for out, first in ((keep_out, me), (give_out, 1 - me)):
            out[at, :half] = jnp.where(first == 0, parts[0][0], parts[1][0]).astype(BF)
            out[at, half:] = jnp.where(first == 0, parts[0][1], parts[1][1]).astype(BF)


def back_kernel(
    steps, sub, cot_ref, ohr_ref, y_ref, sp_ref, rec_ref, oht_ref, gg_ref, wo_ref, ws_ref,
    ed_out, epd_out, far_out, cs_out, cs,
):
    step = pl.program_id(0)
    tile = cot_ref.shape[0]

    @pl.when(step == 0)
    def _():
        cs[...] = jnp.zeros_like(cs)

    for lo in range(0, tile, sub):
        here = slice(lo, lo + sub)
        total = cot_ref[here, :].astype(F32) + dot(ohr_ref[here, :], gg_ref[...])
        ed = norm_grad(y_ref[here, :].astype(F32), rec_ref[here, :], total).astype(BF)
        ed_out[here, :] = ed
        epd_out[here, :] = (dot_nt(ed, wo_ref[...]) * sp_ref[here, :].astype(F32)).astype(BF)
    cs[...] += dot(oht_ref[...], epd_out[...])

    @pl.when(step == steps - 1)
    def _():
        sums = cs[...].astype(BF)
        cs_out[...] = sums
        far_out[:, :D] = dot_nt(sums, ws_ref[...]).astype(BF)


def add_kernel(big_ref, keep_ref, got_ref, out):
    out[...] = (keep_ref[...].astype(F32) + got_ref[...].astype(F32)).astype(BF)


def rest_kernel(
    steps, core_ref, edge_ref, epd_ref, hid_ref, ed_ref, ohtl_ref, ohrt_ref,
    node_ref, n0, n1, n2, n3, far_ref, cs_ref, ws_ref, wr_ref, ntot_ref,
    ntot_out, b0, b1, b2, b3, keep_out, give_out,
    csl, rs, dwe, dwo, g_in, g_out,
):
    step = pl.program_id(0)
    rows = node_ref.shape[0]
    width = n0.shape[0]

    @pl.when(step == 0)
    def _():
        for ref in (csl, rs, dwe, dwo):
            ref[...] = jnp.zeros_like(ref)

    epd = epd_ref[...]
    csl[...] += dot(ohtl_ref[...], epd)
    rs[...] += dot(ohrt_ref[...], epd)
    dwe[...] += dot_tn(edge_ref[...], epd)
    dwo[...] += dot_tn(hid_ref[...], ed_ref[...])

    @pl.when(step == steps - 1)
    def _():
        node = node_ref[...]
        ws = ws_ref[...]
        loc = csl[:rows, :].astype(BF)
        recv = rs[...].astype(BF)
        ntot_out[...] = ntot_ref[...] + dot_nt(loc, ws) + dot_nt(recv, wr_ref[...])
        dws = dot_tn(node, loc) + dot_tn(far_ref[...], cs_ref[...])
        for k, (ref, back) in enumerate(zip((n0, n1, n2, n3), (b0, b1, b2, b3))):
            part = csl[rows + k * width : rows + (k + 1) * width, :].astype(BF)
            back[...] = dot_nt(part, ws).astype(BF)
            dws = dws + dot_tn(ref[...], part)
        g_in[:D, :] = dwe[...].astype(BF)
        g_in[D : 2 * D, :] = dws.astype(BF)
        g_in[2 * D :, :] = dot_tn(node, recv).astype(BF)
        g_out[...] = dwo[...].astype(BF)
        pack_rows(core_ref[0], g_in, g_out, keep_out, give_out)


def pack_rows(me, g_in, g_out, keep_out, give_out):
    def place(r):
        group = r // 64
        return group, (r % 64) // 8, r % 8

    def select(count, depth, source, ok):
        r = iota((count, depth), 0)
        q = iota((count, depth), 1)
        group, k, s = place(r)
        return hot((source(group, k, s) == q) & ok(s))

    def core_of(half):
        return jnp.where(half == 0, me, 1 - me)

    def whole(s):
        return s >= 0

    def low(s):
        return s < 4

    def high(s):
        return s >= 4

    def edge_whole(g, k, s):
        return 24 * k + 12 * core_of(g) + s

    def edge_split(g, k, s):
        core = core_of(g // 2)
        return jnp.where(
            g % 2 == 0, 24 * k + 12 * core + 8 + s % 4, 192 + 8 * k + 4 * core + s % 4
        )

    e_all = select(128, 256, edge_whole, whole)
    e_low = select(256, 256, edge_split, low)
    e_high = select(256, 256, edge_split, high)
    half = D // 2
    for b in range(8):
        edge = jnp.concatenate(
            [g_in[192 * b : 192 * (b + 1), :], g_out[64 * b : 64 * (b + 1), :]], 0
        )
        ew = dot(e_all, edge).astype(BF)
        es = (dot(e_low, edge[:, :half]) + dot(e_high, edge[:, half:])).astype(BF)
        at = slice(64 * b, 64 * (b + 1))
        for i, out in enumerate((keep_out, give_out)):
            out[at, 0:D] = ew[64 * i : 64 * (i + 1), :]
            out[at, D : D + half] = es[128 * i : 128 * i + 64, :]
            out[at, D + half :] = es[128 * i + 64 : 128 * i + 128, :]


def edge_kernel(cot_ref, ohr_ref, epd_ref, gg_ref, we_ref, out):
    total = cot_ref[...].astype(F32) + dot(ohr_ref[...], gg_ref[...])
    out[...] = (total + dot_nt(epd_ref[...], we_ref[...])).astype(BF)


def pair_kernel(keep_ref, got_ref, out):
    out[...] = (keep_ref[...].astype(F32) + got_ref[...].astype(F32)).astype(BF)


def owner_kernel(node_scale, got_ref, ntot_ref, near_ref, far_ref, b0, b1, b2, b3, o2, o3, gn_out):
    rows = ntot_ref.shape[0]
    count = got_ref.shape[0]
    half, quarter = D // 2, D // 4
    sums = jnp.sum(got_ref[:, D:].astype(F32).reshape(count // 16, 16, NG), 0) * node_scale
    for h in range(2):
        part = sums[8 * h : 8 * (h + 1), :]
        o2[:, half * h : half * (h + 1)] = part[:, :half]
        o3[:, half * h : half * h + quarter] = part[0:4, half:]
        o3[:, half * h + quarter : half * (h + 1)] = part[4:8, half:]
    total = ntot_ref[...]
    near = near_ref[0]
    for k, ref in enumerate((b0, b1, b2, b3)):
        total = total + dot(hot(near[k : k + 1, :] == iota((rows, near.shape[1]), 0)), ref[...])
    owner = row_of(far_ref[...], count, lambda g: g)
    total = total + dot(hot(owner == iota((rows, count), 0)), got_ref[:, :D])
    gn_out[...] = total.astype(BF)


def edge_sum_kernel(edge_scale, got_ref, o0, o1):
    half = D // 2
    chips = got_ref.shape[0] // 8
    sums = jnp.sum(got_ref[...].astype(F32).reshape(chips, 8, EG), 0) * edge_scale
    o0[0:8, :] = sums[:, :D]
    o0[8:12, :half] = sums[0:4, D : D + half]
    o0[8:12, half:] = sums[4:8, D : D + half]
    o1[:, :half] = sums[0:4, D + half :]
    o1[:, half:] = sums[4:8, D + half :]


def shards(
    node_latent, edge_latent, node_cotangent, edge_cotangent,
    w_edge_in, w_edge_out, w_node_in, w_node_out,
    sender_code, receiver, near_list, far_list,
):
    rows, width = node_latent.shape
    edges = edge_latent.shape[0]
    n_row, n_col = lax.axis_size("row"), lax.axis_size("col")
    peers = n_row * n_col
    chips = peers // 2
    near_w = near_list.shape[2]
    far_w = far_list.shape[2]
    n_near, n_far = 4 * near_w, peers * far_w
    codes = rows + n_near + n_far
    tile = TILE
    steps = edges // tile
    sds = jax.ShapeDtypeStruct
    far_t = jnp.swapaxes(far_list[0], 0, 1)
    core = (lax.axis_index("col") % 2).astype(jnp.int32).reshape(1)
    smem = pl.BlockSpec(memory_space=pltpu.SMEM)

    *near_send, far_send = pl.pallas_call(
        offer_kernel,
        out_shape=(*[sds((near_w, width), BF)] * 4, sds((n_far, width), BF)),
        compiler_params=params(0),
        name="offer",
    )(node_latent, near_list, far_t)

    far = lax.all_to_all(far_send.reshape(peers, far_w, width), AXES, 0, 0, tiled=True)
    far = far.reshape(n_far, width)
    moves = (("row", 1), ("row", -1), ("col", 1), ("col", -1))

    def shifted(value, axis, by):
        n = lax.axis_size(axis)
        return lax.ppermute(value, axis, [(i, (i + by) % n) for i in range(n)])

    near = [shifted(part, axis, by) for part, (axis, by) in zip(near_send, moves)]

    def rowed(cols):
        return pl.BlockSpec((tile, cols), lambda s: (s, 0))

    def laned(lead):
        return pl.BlockSpec((lead, tile), lambda s: (0, s))

    def wpart(k):
        return pl.BlockSpec((width, width), lambda *_: (k, 0), pipeline_mode=pl.Buffered(1))

    def once(shape):
        return pl.BlockSpec(shape, lambda *_: (0,) * len(shape), pipeline_mode=pl.Buffered(1))

    blocks = full((edges // 128, 128))
    pre_local, oh, oht, ohr, ohrt = pl.pallas_call(
        functools.partial(local_kernel, rows),
        grid=(steps,),
        in_specs=[
            rowed(width), once((rows, width)), wpart(0), wpart(1), wpart(2),
            blocks, laned(1), blocks, laned(1),
        ],
        out_specs=[rowed(width), rowed(codes - rows), laned(codes), rowed(rows), laned(rows)],
        out_shape=(
            sds((edges, width), F32),
            sds((edges, codes - rows), BF),
            sds((codes, edges), BF),
            sds((edges, rows), BF),
            sds((rows, edges), BF),
        ),
        scratch_shapes=[pltpu.VMEM((rows, width), BF), pltpu.VMEM((rows, width), BF)],
        compiler_params=params(),
        cost_estimate=cost(2 * edges * width * (width + 2 * rows), 22e6),
        name="local",
    )(
        edge_latent, node_latent, w_edge_in, w_edge_in, w_edge_in,
        sender_code.reshape(edges // 128, 128), sender_code.reshape(1, edges),
        receiver.reshape(edges // 128, 128), receiver.reshape(1, edges),
    )

    near_spec = [once((near_w, width))] * 4
    node_spec = once((rows, width))
    sq = once((width, width))
    packed = once((8 * peers, NG))
    edge_bf = sds((edges, width), BF)
    edge_new, y, sp, hid, rec, node_new, gg, ntot, keep_n, give_n = pl.pallas_call(
        functools.partial(forward_kernel, steps, SUB),
        grid=(steps,),
        in_specs=[
            smem, rowed(width), rowed(codes - rows), rowed(width), laned(rows),
            *near_spec, once((n_far, width)), wpart(1), sq,
            node_spec, node_spec, wpart(0), wpart(1), sq,
        ],
        out_specs=[
            rowed(width), rowed(width), rowed(width), rowed(width), rowed(1),
            node_spec, node_spec, node_spec, packed, packed,
        ],
        out_shape=(
            edge_bf, edge_bf, edge_bf, edge_bf, sds((edges, 1), F32),
            sds((rows, width), BF), sds((rows, width), BF), sds((rows, width), F32),
            sds((8 * peers, NG), BF), sds((8 * peers, NG), BF),
        ),
        scratch_shapes=[
            pltpu.VMEM((codes - rows, width), BF),
            pltpu.VMEM((rows, width), F32),
            pltpu.VMEM((2 * width, width), BF),
            pltpu.VMEM((width, width), BF),
        ],
        compiler_params=params(),
        cost_estimate=cost(9e9, 24e6),
        name="forward",
    )(
        core, pre_local, oh, edge_latent, ohrt,
        *near, far, w_edge_in, w_edge_out,
        node_latent, node_cotangent, w_node_in, w_node_in, w_node_out,
    )

    def to_pair(value):
        return lax.ppermute(value, "col", [(i, i ^ 1) for i in range(n_col)])

    backward = pl.pallas_call(
        functools.partial(back_kernel, steps, SUB),
        grid=(steps,),
        in_specs=[
            rowed(width), rowed(rows), rowed(width), rowed(width), rowed(1),
            pl.BlockSpec(
                (pl.Element(n_far), pl.Element(tile)), lambda s: (rows + n_near, s * tile)
            ),
            node_spec, sq, wpart(1),
        ],
        out_specs=[
            rowed(width), rowed(width), once((n_far, width + NG)), once((n_far, width)),
        ],
        out_shape=(
            edge_bf, edge_bf, sds((n_far, width + NG), BF), sds((n_far, width), BF),
        ),
        scratch_shapes=[pltpu.VMEM((n_far, width), F32)],
        compiler_params=params(),
        cost_estimate=cost(6e9, 22e6),
        name="backward",
    )
    got_n = to_pair(give_n)
    ed, epd, far_grad, cs_far = backward(
        edge_cotangent, ohr, y, sp, rec, oht, gg, w_edge_out, w_edge_in
    )
    lanes = pl.BlockSpec((n_far, 128), lambda s: (0, s))
    beyond = pl.BlockSpec((n_far, 128), lambda s: (0, s + width // 128))
    sent = pl.pallas_call(
        add_kernel,
        grid=(NG // 128,),
        in_specs=[pl.BlockSpec(memory_space=pl.ANY), lanes, lanes],
        out_specs=beyond,
        out_shape=sds((n_far, width + NG), BF),
        input_output_aliases={0: 0},
        compiler_params=params(),
        name="add",
    )(far_grad, keep_n, got_n)
    rest = pl.pallas_call(
        functools.partial(rest_kernel, steps),
        grid=(steps,),
        in_specs=[
            smem, rowed(width), rowed(width), rowed(width), rowed(width),
            laned(rows + n_near), laned(rows),
            node_spec, *near_spec, once((n_far, width)), once((n_far, width)),
            wpart(1), wpart(2), node_spec,
        ],
        out_specs=[node_spec, *near_spec, once((8 * chips, EG)), once((8 * chips, EG))],
        out_shape=(
            sds((rows, width), F32), *[sds((near_w, width), BF)] * 4,
            sds((8 * chips, EG), BF), sds((8 * chips, EG), BF),
        ),
        scratch_shapes=[
            pltpu.VMEM((rows + n_near, width), F32),
            pltpu.VMEM((rows, width), F32),
            pltpu.VMEM((width, width), F32),
            pltpu.VMEM((width, width), F32),
            pltpu.VMEM((3 * width, width), BF),
            pltpu.VMEM((width, width), BF),
        ],
        compiler_params=params(),
        cost_estimate=cost(7e9, 14e6),
        name="rest",
    )
    returned = lax.all_to_all(sent.reshape(peers, far_w, width + NG), AXES, 0, 0, tiled=True)
    ntot, b0, b1, b2, b3, keep, give = rest(
        core, edge_latent, epd, hid, ed, oht, ohrt, node_latent, *near, far, cs_far,
        w_edge_in, w_edge_in, ntot,
    )

    edges_of = pl.pallas_call(
        edge_kernel,
        grid=(steps,),
        in_specs=[rowed(width), rowed(rows), rowed(width), node_spec, wpart(0)],
        out_specs=rowed(width),
        out_shape=sds((edges, width), BF),
        compiler_params=params(),
        cost_estimate=cost(6e9, 9e6),
        name="edges",
    )
    got = to_pair(give)
    back = [shifted(b, axis, -by) for b, (axis, by) in zip((b0, b1, b2, b3), moves)]
    grad_edge = edges_of(edge_cotangent, ohr, epd, gg, w_edge_in)

    part = pl.BlockSpec((2 * chips, EG), lambda s: (s, 0))
    pair = pl.pallas_call(
        pair_kernel,
        grid=(4,),
        in_specs=[part, part],
        out_specs=part,
        out_shape=sds((8 * chips, EG), BF),
        compiler_params=params(),
        name="pair",
    )(keep, got)
    same_core = [[2 * i + c for i in range(chips)] for c in range(2)]
    vm = pl.BlockSpec(memory_space=pltpu.VMEM)
    edge_scale = 1.0 / math.sqrt(edges * peers)
    node_scale = 1.0 / math.sqrt(rows * peers)
    parts = lax.all_to_all(
        pair.reshape(chips, 8, EG), AXES, 0, 0, axis_index_groups=same_core, tiled=True
    )
    g2, g3, grad_node = pl.pallas_call(
        functools.partial(owner_kernel, node_scale),
        in_specs=[vm] * 8,
        out_specs=[vm] * 3,
        out_shape=(
            sds((8, width), F32), sds((4, width), F32), sds((rows, width), BF),
        ),
        compiler_params=params(0),
        cost_estimate=cost(4e8, 5e6),
        name="owner",
    )(returned.reshape(n_far, width + NG), ntot, near_list, far_t, *back)
    g0, g1 = pl.pallas_call(
        functools.partial(edge_sum_kernel, edge_scale),
        in_specs=[vm],
        out_specs=[vm] * 2,
        out_shape=(sds((12, width), F32), sds((4, width), F32)),
        compiler_params=params(0),
        name="edgesum",
    )(parts.reshape(8 * chips, EG))
    return (node_new, edge_new, grad_node, grad_edge, g0, g1, g2, g3)


def solution(mesh):
    both = P(AXES, None)
    in_specs = (
        both, both, both, both, P(), P(), P(), P(), P(AXES), P(AXES),
        P(AXES, None, None), P(AXES, None, None),
    )
    return jax.shard_map(
        shards, mesh=mesh, in_specs=in_specs, out_specs=(both,) * 8, check_vma=False
    )
```

time: 154 us -> 150 us (0.974); the launches traced: 152 us -> 150 us
  Pallas kernels: 63.2 us -> 77.3 us
  local copies, waits for them, and re-layouts: 9.46 us -> 0.01 us
  other arithmetic: 3.54 us -> 0 us
  waiting for transfers between devices: 35 us -> 32.4 us
    pallas_call x5 -> x9, Pallas kernels: 52.3 us -> 67.2 us  [the longest x1 19 us: shards(): pl.pallas_call(functools.partial(forward_kernel, steps, SUB), grid=(steps...]
    ppermute x8, waiting for transfers between devices: 16.9 us -> 9.95 us  [shifted(): return lax.ppermute(value, axis, [(i, (i + by) % n) for i in range(n)])]
    unnamed x39 -> x2, local copies, waits for them, and re-layouts: 5.42 us -> 0.01 us
    ppermute x1 -> x2, waiting for transfers between devices: 0.01 us -> 5.27 us  [to_pair(): return lax.ppermute(value, 'col', [(i, i ^ 1) for i in range(n_col)])]
    reshape x4 -> x0, local copies, waits for them, and re-layouts: 4.02 us -> none  [the longest x1 1.35 us: shards(): recv_c = receiver.reshape(edges, 1)]
    convert_element_type x1 -> x0, other arithmetic: 3.54 us -> none  [shards(): (keep.astype(F32) + got.astype(F32)).astype(BF)]
    all_to_all x2, starting transfers between devices: 14.4 us -> 11.4 us  [the longest x1 5.71 us: shards(): lax.all_to_all(sent.reshape(peers, far_w, width + NG), AXES, 0, 0, tiled=...]
    ppermute x8, starting transfers between devices: 14 us -> 15.7 us  [shifted(): return lax.ppermute(value, axis, [(i, (i + by) % n) for i in range(n)])]
  transfers between devices with their start and end apart: 12 -> 13, of which waited for: 6 -> 7; matrix products, arithmetic and copies ran while one was open for 5% -> 0% of each run, Pallas kernels for 9% -> 14%
where the time goes in v2:
time: 150 us
  Pallas kernels  77.3 us (52%)
  starting transfers between devices  39.1 us (26%)
  waiting for transfers between devices  32.4 us (22%)
    pallas_call x1, Pallas kernels, shards(): pl.pallas_call(functools.partial(forward_kernel, steps, SUB), grid=(steps...  19 us
    ppermute x8, starting transfers between devices, shifted(): return lax.ppermute(value, axis, [(i, (i + by) % n) for i in range(n)])  15.7 us
    pallas_call x1, Pallas kernels, shards(): backward(edge_cotangent, ohr, y, sp, rec, oht, gg, w_edge_out, w_edge_in)  14 us
    all_to_all x1, waiting for transfers between devices, shards(): lax.all_to_all(pair.reshape(chips, 8, EG), AXES, 0, 0, axis_index_groups=...  13.7 us
    pallas_call x1, Pallas kernels, shards(): rest(core, edge_latent, epd, hid, ed, oht, ohrt, node_latent, *near, far,...  13.7 us
    all_to_all x1, starting transfers between devices, shards(): lax.all_to_all(far_send.reshape(peers, far_w, width), AXES, 0, 0, tiled=T...  11.7 us
    pallas_call x1, Pallas kernels, shards(): pl.pallas_call(functools.partial(local_kernel, rows), grid=(steps,), in_s...  10.1 us
    ppermute x8, waiting for transfers between devices, shifted(): return lax.ppermute(value, axis, [(i, (i + by) % n) for i in range(n)])  9.95 us
  transfers between devices with their start and end apart: 13, of which 7 were waited for; matrix products, arithmetic and copies ran while one was open for 0% of the time, Pallas kernels for 14%

profile of v2, /device:TPU:0, one launch (start us, length us, event | category | flops | bytes accessed | tf_op | source)
XLA Modules:
  0.0 149.5 jit_solution(18356616050435786161)
XLA Ops:
  0.6 2.8 %offer.1 = (bf16[64,512]{1,0:T(8,128)(2,1)}, bf16[64,512]{1,0:T(8,128)(2,1)}, bf16[64,512]{1,0:T(8,128)(2,1)}, bf16[64,512]{1,0:T(8,128)(2,1)}, bf16[1024,512]{1,0:T(8,128)(2,1)}) custom-call(bf16[256,512]{1,0:T(8,128)(2,1)} %node_ref.7, s32[1,4,64]{2,1,0:T(4,128)} %near_ref.3, s32[8,128]{1,0:T(8,128)} %bitcast.17), custom_call_target="tpu_custom_call" | custom-call | tf_op jit(solution)/shard_map/offer/pallas_call | solution.py:398
  3.4 11.7 %all-to-all-start = ((bf16[128,8,512]{2,1,0:T(8,128)(2,1)}), bf16[128,8,512]{2,1,0:T(8,128)(2,1)}, u32[]{:S(2)}, u32[]{:S(2)}) async-start(bf16[128,8,512]{2,1,0:T(8,128)(2,1)} %bitcast.16), calls=%async_computation | async-start | bytes 2097152 | tf_op jit(solution)/shard_map/all_to_all | solution.py:405
  15.1 1.1 collective-permute-start
  16.2 4.3 %collective-permute-start.1 = (bf16[64,512]{1,0:T(8,128)(2,1)}, bf16[64,512]{1,0:T(8,128)(2,1)}, u32[]{:S(2)}, u32[]{:S(2)}) collective-permute-start(bf16[64,512]{1,0:T(8,128)(2,1)} %get-tuple-element.48), channel_id=1, source_target_pairs={{0,120},{8,0},{16,8},{24,16},{32,24},{40,32},{48,40},{56,48},{64,5... | collective-permute-start | bytes 196616 | tf_op jit(solution)/shard_map/ppermute | solution.py:411
  20.5 3.0 %collective-permute-start.3 = (bf16[64,512]{1,0:T(8,128)(2,1)}, bf16[64,512]{1,0:T(8,128)(2,1)}, u32[]{:S(2)}, u32[]{:S(2)}) collective-permute-start(bf16[64,512]{1,0:T(8,128)(2,1)} %get-tuple-element.50), channel_id=1, source_target_pairs={{0,7},{1,0},{2,1},{3,2},{4,3},{5,4},{6,5},{7,6},{8,15},{9,8},{10,9... | collective-permute-start | bytes 196616 | tf_op jit(solution)/shard_map/ppermute | solution.py:411
  23.5 10.1 %local.1 = (f32[2048,512]{1,0:T(8,128)}, bf16[2048,1280]{1,0:T(8,128)(2,1)}, bf16[1536,2048]{1,0:T(8,128)(2,1)}, bf16[2048,256]{1,0:T(8,128)(2,1)}, bf16[256,2048]{1,0:T(8,128)(2,1)}) custom-call(bf16[2048,512]{1,0:T(8,128)(2,1)} %edge_ref.5, bf16[256,512]{1,0:T(8,128)(2,1)} %node_ref.7, bf16[1536,512]{1,0:T(8,128)(2,1)} %we_ref.3, ...), custom_call_target="tpu_custom_call" | custom-call | flops 2147483648 | bytes 22000000 | tf_op jit(solution)/shard_map/local/pallas_call | solution.py:428
  34.4 19.0 %forward.1 = (bf16[2048,512]{1,0:T(8,128)(2,1)}, bf16[2048,512]{1,0:T(8,128)(2,1)}, bf16[2048,512]{1,0:T(8,128)(2,1)}, bf16[2048,512]{1,0:T(8,128)(2,1)}, f32[20...) custom-call(s32[1]{0:T(128)} %bitcast.core_ref, ...), custom_call_target="tpu_custom_call" | custom-call | flops 8999999488 | bytes 24000000 | tf_op jit(solution)/shard_map/forward/pallas_call | solution.py:458
  53.4 14.0 %backward.1 = (bf16[2048,512]{1,0:T(8,128)(2,1)}, bf16[2048,512]{1,0:T(8,128)(2,1)}, bf16[1024,896]{1,0:T(8,128)(2,1)}, bf16[1024,512]{1,0:T(8,128)(2,1)}) custom-call(bf16[2048,512]{1,0:T(8,128)(2,1)} %cot_ref.3, bf16[2048,256]{1,0:T(8,128)(2,1)} %get-tuple-element.54.ohr_ref, bf16[2048,512]{1,0:T(8,128)(2,1)} %get-tuple-element.55.y_ref, ...), custom_call_target="tpu_custom_call" | custom-call | flops 6000000000 | bytes 22000000 | tf_op jit(solution)/shard_map/backward/pallas_call | solution.py:515
  67.4 13.7 %rest.1 = (f32[256,512]{1,0:T(8,128)}, bf16[64,512]{1,0:T(8,128)(2,1)}, bf16[64,512]{1,0:T(8,128)(2,1)}, bf16[64,512]{1,0:T(8,128)(2,1)}, bf16[64,512]{1,0:T(8,1...) custom-call(s32[1]{0:T(128)} %bitcast.core_ref, bf16[2048,512]{1,0:T(8,128)(2,1)} %edge_ref.5, ...), custom_call_target="tpu_custom_call" | custom-call | flops 7000000000 | bytes 14000000 | tf_op jit(solution)/shard_map/rest/pallas_call | solution.py:557
  81.2 3.0 %collective-permute-done.9.got_ref = bf16[512,1024]{1,0:T(8,128)(2,1)} collective-permute-done((bf16[512,1024]{1,0:T(8,128)(2,1)}, bf16[512,1024]{1,0:T(8,128)(2,1)}, u32[]{:S(2)}, u32[]{:S(2)}) %collective-permute-start.9) | collective-permute-done | bytes 1048608 | tf_op jit(solution)/shard_map/ppermute | solution.py:491
  84.2 3.6 %pair.1 = bf16[512,1024]{1,0:T(8,128)(2,1)} custom-call(bf16[512,1024]{1,0:T(8,128)(2,1)} %get-tuple-element.74.keep_ref, bf16[512,1024]{1,0:T(8,128)(2,1)} %collective-permute-done.9.got_ref), custom_call_target="tpu_custom_call" | custom-call | tf_op jit(solution)/shard_map/pair/pallas_call | solution.py:577
  87.8 5.6 %all-to-all-start.2 = ((bf16[64,8,1024]{2,1,0:T(8,128)(2,1)}), bf16[64,8,1024]{2,1,0:T(8,128)(2,1)}, u32[]{:S(2)}, u32[]{:S(2)}) async-start(bf16[64,8,1024]{2,1,0:T(8,128)(2,1)} %bitcast.15), calls=%async_computation.2 | async-start | bytes 2097152 | tf_op jit(solution)/shard_map/all_to_all | solution.py:590
  93.7 2.3 %collective-permute-done.4.got_ref = bf16[1024,384]{1,0:T(8,128)(2,1)} collective-permute-done((bf16[1024,384]{1,0:T(8,128)(2,1)S(1)}, bf16[1024,384]{1,0:T(8,128)(2,1)}, u32[]{:S(2)}, u32[]{:S(2)}) %collective-permute-start.4) | collective-permute-done | bytes 786464 | tf_op jit(solution)/shard_map/ppermute | solution.py:491
  95.9 3.1 %add.6 = bf16[1024,896]{1,0:T(8,128)(2,1)} custom-call(bf16[1024,896]{1,0:T(8,128)(2,1)} %get-tuple-element.60.big_ref, bf16[1024,384]{1,0:T(8,128)(2,1)} %get-tuple-element.61.keep_ref, bf16[1024,384]{1,0:T(8,128)(2,1)} %collective-permute-done.4.got_ref), custom_call_target="tpu_custom_call", output_to_operand_aliasing={{}: (0, {})} | custom-call | tf_op jit(solution)/shard_map/add/pallas_call | solution.py:520
  99.1 13.7 %all-to-all-done.2 = bf16[64,8,1024]{2,1,0:T(8,128)(2,1)} async-done(((bf16[64,8,1024]{2,1,0:T(8,128)(2,1)}), bf16[64,8,1024]{2,1,0:T(8,128)(2,1)}, u32[]{:S(2)}, u32[]{:S(2)}) %all-to-all-start.2) | async-done | bytes 1048608 | tf_op jit(solution)/shard_map/all_to_all | solution.py:590
  112.8 5.7 %all-to-all-start.1 = ((bf16[128,8,896]{2,1,0:T(8,128)(2,1)}), bf16[128,8,896]{2,1,0:T(8,128)(2,1)}, u32[]{:S(2)}, u32[]{:S(2)}) async-start(bf16[128,8,896]{2,1,0:T(8,128)(2,1)} %bitcast.14), calls=%async_computation.1 | async-start | bytes 3670016 | tf_op jit(solution)/shard_map/all_to_all | solution.py:556
  118.5 5.1 %collective-permute-start.5 = (bf16[64,512]{1,0:T(8,128)(2,1)}, bf16[64,512]{1,0:T(8,128)(2,1)}, u32[]{:S(2)}, u32[]{:S(2)}) collective-permute-start(bf16[64,512]{1,0:T(8,128)(2,1)} %get-tuple-element.69), channel_id=1, source_target_pairs={{0,120},{8,0},{16,8},{24,16},{32,24},{40,32},{48,40},{56,48},{64,5... | collective-permute-start | bytes 196616 | tf_op jit(solution)/shard_map/ppermute | solution.py:411
  123.7 2.2 %collective-permute-start.7 = (bf16[64,512]{1,0:T(8,128)(2,1)}, bf16[64,512]{1,0:T(8,128)(2,1)}, u32[]{:S(2)}, u32[]{:S(2)}) collective-permute-start(bf16[64,512]{1,0:T(8,128)(2,1)} %get-tuple-element.71), channel_id=1, source_target_pairs={{0,7},{1,0},{2,1},{3,2},{4,3},{5,4},{6,5},{7,6},{8,15},{9,8},{10,9... | collective-permute-start | bytes 196616 | tf_op jit(solution)/shard_map/ppermute | solution.py:411
  125.9 5.7 %edges.1 = bf16[2048,512]{1,0:T(8,128)(2,1)} custom-call(bf16[2048,512]{1,0:T(8,128)(2,1)} %cot_ref.3, bf16[2048,256]{1,0:T(8,128)(2,1)} %get-tuple-element.54.ohr_ref, bf16[2048,512]{1,0:T(8,128)(2,1)} %get-tuple-element.63.epd_ref, bf16[256,512]{1,0:T(8,128)(2,1)} %get-tuple-element.59.gg_ref, bf16[1536,512]{1,0:T(8,128)(2,1)} %we_ref.3), custom_call_target="tpu_custom_call" | custom-call | flops 6000000000 | bytes 9000000 | tf_op jit(solution)/shard_map/edges/pallas_call | solution.py:574
  131.6 2.0 %edgesum.1 = (f32[12,512]{1,0:T(8,128)}, f32[4,512]{1,0:T(4,128)}) custom-call(bf16[512,1024]{1,0:T(8,128)(2,1)} %bitcast.13.got_ref), custom_call_target="tpu_custom_call" | custom-call | tf_op jit(solution)/shard_map/edgesum/pallas_call | solution.py:604
  133.6 5.1 %collective-permute-done.5.b0 = bf16[64,512]{1,0:T(8,128)(2,1)} collective-permute-done((bf16[64,512]{1,0:T(8,128)(2,1)}, bf16[64,512]{1,0:T(8,128)(2,1)}, u32[]{:S(2)}, u32[]{:S(2)}) %collective-permute-start.5) | collective-permute-done | bytes 65568 | tf_op jit(solution)/shard_map/ppermute | solution.py:411
  138.7 4.8 %collective-permute-done.6.b1 = bf16[64,512]{1,0:T(8,128)(2,1)} collective-permute-done((bf16[64,512]{1,0:T(8,128)(2,1)}, bf16[64,512]{1,0:T(8,128)(2,1)}, u32[]{:S(2)}, u32[]{:S(2)}) %collective-permute-start.6) | collective-permute-done | bytes 65568 | tf_op jit(solution)/shard_map/ppermute | solution.py:411
  143.5 2.8 %all-to-all-done.1 = bf16[128,8,896]{2,1,0:T(8,128)(2,1)} async-done(((bf16[128,8,896]{2,1,0:T(8,128)(2,1)}), bf16[128,8,896]{2,1,0:T(8,128)(2,1)}, u32[]{:S(2)}, u32[]{:S(2)}) %all-to-all-start.1) | async-done | bytes 1835040 | tf_op jit(solution)/shard_map/all_to_all | solution.py:556
  146.3 3.3 %owner.1 = (f32[8,512]{1,0:T(8,128)}, f32[4,512]{1,0:T(4,128)}, bf16[256,512]{1,0:T(8,128)(2,1)}) custom-call(bf16[1024,896]{1,0:T(8,128)(2,1)} %bitcast.10.got_ref, f32[256,512]{1,0:T(8,128)} %get-tuple-element.68.ntot_ref, s32[1,4,64]{2,1,0:T(4,128)} %near_ref.3, s32[8,128]{1,0:T(8,128)} %bitcast.18, bf16[64,512]{1,0:T(8,128)(2,1)} %collective-permute-done.5.b0, ...), custom_call_target="tpu_custom_call" | custom-call | flops 400000000 | bytes 5000000 | tf_op jit(solution)/shard_map/owner/pallas_call | solution.py:593
  (14 shorter events, 1.0 us)
Async XLA Ops:
  3.4 31.0 %all-to-all-start = ((bf16[128,8,512]{2,1,0:T(8,128)(2,1)}), bf16[128,8,512]{2,1,0:T(8,128)(2,1)}, u32[]{:S(2)}, u32[]{:S(2)}) async-start(bf16[128,8,512]{2,1,0:T(8,128)(2,1)} %bitcast.16), calls=%async_computation | async-start | bytes 2097152 | tf_op jit(solution)/shard_map/all_to_all | solution.py:405
  15.1 18.5 %collective-permute-start = (bf16[64,512]{1,0:T(8,128)(2,1)}, bf16[64,512]{1,0:T(8,128)(2,1)}, u32[]{:S(2)}, u32[]{:S(2)}) collective-permute-start(bf16[64,512]{1,0:T(8,128)(2,1)} %get-tuple-element.47), channel_id=1, source_target_pairs={{0,8},{8,16},{16,24},{24,32},{32,40},{40,48},{48,56},{56,64},{64,7... | collective-permute-start | bytes 196616 | tf_op jit(solution)/shard_map/ppermute | solution.py:411
  16.2 17.5 %collective-permute-start.1 = (bf16[64,512]{1,0:T(8,128)(2,1)}, bf16[64,512]{1,0:T(8,128)(2,1)}, u32[]{:S(2)}, u32[]{:S(2)}) collective-permute-start(bf16[64,512]{1,0:T(8,128)(2,1)} %get-tuple-element.48), channel_id=1, source_target_pairs={{0,120},{8,0},{16,8},{24,16},{32,24},{40,32},{48,40},{56,48},{64,5... | collective-permute-start | bytes 196616 | tf_op jit(solution)/shard_map/ppermute | solution.py:411
  20.5 13.1 %collective-permute-start.2 = (bf16[64,512]{1,0:T(8,128)(2,1)}, bf16[64,512]{1,0:T(8,128)(2,1)}, u32[]{:S(2)}, u32[]{:S(2)}) collective-permute-start(bf16[64,512]{1,0:T(8,128)(2,1)} %get-tuple-element.49), channel_id=1, source_target_pairs={{0,1},{1,2},{2,3},{3,4},{4,5},{5,6},{6,7},{7,0},{8,9},{9,10},{10,1... | collective-permute-start | bytes 196616 | tf_op jit(solution)/shard_map/ppermute | solution.py:411
  20.5 13.1 %collective-permute-start.3 = (bf16[64,512]{1,0:T(8,128)(2,1)}, bf16[64,512]{1,0:T(8,128)(2,1)}, u32[]{:S(2)}, u32[]{:S(2)}) collective-permute-start(bf16[64,512]{1,0:T(8,128)(2,1)} %get-tuple-element.50), channel_id=1, source_target_pairs={{0,7},{1,0},{2,1},{3,2},{4,3},{5,4},{6,5},{7,6},{8,15},{9,8},{10,9... | collective-permute-start | bytes 196616 | tf_op jit(solution)/shard_map/ppermute | solution.py:411
  81.1 3.1 %collective-permute-start.9 = (bf16[512,1024]{1,0:T(8,128)(2,1)}, bf16[512,1024]{1,0:T(8,128)(2,1)}, u32[]{:S(2)}, u32[]{:S(2)}) collective-permute-start(bf16[512,1024]{1,0:T(8,128)(2,1)} %get-tuple-element.75), channel_id=1, source_target_pairs={{0,1},{1,0},{2,3},{3,2},{4,5},{5,4},{6,7},{7,6},{8,9},{9,8},{10,11... | collective-permute-start | bytes 3145736 | tf_op jit(solution)/shard_map/ppermute | solution.py:491
  87.8 5.7 %copy-start = (bf16[1024,384]{1,0:T(8,128)(2,1)S(1)}, bf16[1024,384]{1,0:T(8,128)(2,1)}, u32[]{:S(2)}) copy-start(bf16[1024,384]{1,0:T(8,128)(2,1)} %get-tuple-element.62) | copy-start | bytes 2359300
  87.8 25.0 %all-to-all-start.2 = ((bf16[64,8,1024]{2,1,0:T(8,128)(2,1)}), bf16[64,8,1024]{2,1,0:T(8,128)(2,1)}, u32[]{:S(2)}, u32[]{:S(2)}) async-start(bf16[64,8,1024]{2,1,0:T(8,128)(2,1)} %bitcast.15), calls=%async_computation.2 | async-start | bytes 2097152 | tf_op jit(solution)/shard_map/all_to_all | solution.py:590
  93.5 2.5 %collective-permute-start.4 = (bf16[1024,384]{1,0:T(8,128)(2,1)S(1)}, bf16[1024,384]{1,0:T(8,128)(2,1)}, u32[]{:S(2)}, u32[]{:S(2)}) collective-permute-start(bf16[1024,384]{1,0:T(8,128)(2,1)S(1)} %copy-done), channel_id=1, source_target_pairs={{0,1},{1,0},{2,3},{3,2},{4,5},{5,4},{6,7},{7,6},{8,9},{9,8},{10,11... | collective-permute-start | bytes 2359304 | tf_op jit(solution)/shard_map/ppermute | solution.py:491
  112.8 33.5 %all-to-all-start.1 = ((bf16[128,8,896]{2,1,0:T(8,128)(2,1)}), bf16[128,8,896]{2,1,0:T(8,128)(2,1)}, u32[]{:S(2)}, u32[]{:S(2)}) async-start(bf16[128,8,896]{2,1,0:T(8,128)(2,1)} %bitcast.14), calls=%async_computation.1 | async-start | bytes 3670016 | tf_op jit(solution)/shard_map/all_to_all | solution.py:556
  118.5 20.1 %collective-permute-start.5 = (bf16[64,512]{1,0:T(8,128)(2,1)}, bf16[64,512]{1,0:T(8,128)(2,1)}, u32[]{:S(2)}, u32[]{:S(2)}) collective-permute-start(bf16[64,512]{1,0:T(8,128)(2,1)} %get-tuple-element.69), channel_id=1, source_target_pairs={{0,120},{8,0},{16,8},{24,16},{32,24},{40,32},{48,40},{56,48},{64,5... | collective-permute-start | bytes 196616 | tf_op jit(solution)/shard_map/ppermute | solution.py:411
  123.7 19.8 %collective-permute-start.6 = (bf16[64,512]{1,0:T(8,128)(2,1)}, bf16[64,512]{1,0:T(8,128)(2,1)}, u32[]{:S(2)}, u32[]{:S(2)}) collective-permute-start(bf16[64,512]{1,0:T(8,128)(2,1)} %get-tuple-element.70), channel_id=1, source_target_pairs={{0,8},{8,16},{16,24},{24,32},{32,40},{40,48},{48,56},{56,64},{64,7... | collective-permute-start | bytes 196616 | tf_op jit(solution)/shard_map/ppermute | solution.py:411
  123.7 19.8 %collective-permute-start.7 = (bf16[64,512]{1,0:T(8,128)(2,1)}, bf16[64,512]{1,0:T(8,128)(2,1)}, u32[]{:S(2)}, u32[]{:S(2)}) collective-permute-start(bf16[64,512]{1,0:T(8,128)(2,1)} %get-tuple-element.71), channel_id=1, source_target_pairs={{0,7},{1,0},{2,1},{3,2},{4,3},{5,4},{6,5},{7,6},{8,15},{9,8},{10,9... | collective-permute-start | bytes 196616 | tf_op jit(solution)/shard_map/ppermute | solution.py:411
  125.9 17.7 %collective-permute-start.8 = (bf16[64,512]{1,0:T(8,128)(2,1)}, bf16[64,512]{1,0:T(8,128)(2,1)}, u32[]{:S(2)}, u32[]{:S(2)}) collective-permute-start(bf16[64,512]{1,0:T(8,128)(2,1)} %get-tuple-element.72), channel_id=1, source_target_pairs={{0,1},{1,2},{2,3},{3,4},{4,5},{5,6},{6,7},{7,0},{8,9},{9,10},{10,1... | collective-permute-start | bytes 196616 | tf_op jit(solution)/shard_map/ppermute | solution.py:411
